TPU v7x, 256 devices: a whole 4x4x8 slice. The times are simulated.
256 devices in a mesh: dp: 128 (over y, z, x), mp: 2 (over core).
Axes of the slice: x: 4, y: 4, z: 8, core: 2. Of those that a mesh axis runs over, the one named last changes fastest.
Arguments:
- grad: bfloat16 [32, 1024, 8192], P(None, 'dp', 'mp'), may hold values from -6 to 6
- second_moment: float32 [32, 1024, 8192], P(None, 'dp', 'mp'), may hold values from 0.004 to 20, as said below
- left_root: bfloat16 [2, 128, 1024, 1024], P('mp', 'dp'), as said below
- right_root: bfloat16 [2, 128, 1024, 1024], P('mp', 'dp'), as said below
- owner_slot: int32 [2, 32, 4], replicated, may hold values from 0 to 127, as said below
Outputs:
- update: bfloat16 [32, 1024, 8192], P(None, 'dp', 'mp')
Inputs may be any that keep to these rules, and one draw needn't show every extreme that they name: For each h, owner_slot[h] lists every dp index exactly once: each dp index owns one block of each h. `second_moment`: positive. `left_root`: each square is symmetric positive definite. `right_root`: each square is symmetric positive definite.
All inputs are finite; a program needn't handle non-finite values.
Results may differ from a plain program's by a relative error of at most 0.0049.
Values may be sent and summed in bfloat16 or wider, within the bound.
No kernel may reach another device: no remote copies, remote signals or barrier semaphores. Data moves between devices by JAX's collectives and lax.ppermute only.
A program may use at most 64 MiB of HBM per device.

v0:
```python
import jax
import jax.numpy as jnp
from jax import lax
from jax.sharding import Mesh
from jax.sharding import PartitionSpec as P

DP = ("dp_0", "dp_1", "dp_2")


BETA_TWO = 0.99
ADAM_EPS = 1e-08
NORM_EPS = 1e-06


def one_axis_at_a_time(value, axes):
    for axis in axes:
        value = lax.psum(value, axis)
    return value


def per_device(grad, second_moment, left_root, right_root, owner_slot):
    row_blocks, block_rows, half_cols = grad.shape
    block_size = left_root.shape[-1]
    col_blocks = half_cols // block_size
    dp_count = lax.axis_size(DP)
    mp_index = lax.axis_index("mp")
    owner_index = lax.axis_index(DP)
    widened = grad.astype(jnp.float32)
    moment_new = BETA_TWO * second_moment + (1.0 - BETA_TWO) * widened * widened
    direction = widened / (jnp.sqrt(moment_new) + ADAM_EPS)
    partial_value = jnp.sum(
        (direction * direction).reshape(row_blocks, block_rows, col_blocks, block_size), axis=(1, 3)
    )
    table = lax.dynamic_index_in_dim(owner_slot, mp_index, 0, keepdims=False)
    owner_ids = lax.iota(jnp.int32, dp_count)
    matches = table[None, :, :] == owner_ids[:, None, None]
    select_half = matches.astype(jnp.bfloat16)
    select_full = matches.astype(jnp.float32).reshape(dp_count, row_blocks * col_blocks)
    tiles = grad.reshape(row_blocks, block_rows, col_blocks, block_size)
    outgoing = jnp.einsum("src,rwck->swk", select_half, tiles, preferred_element_type=jnp.float32)
    outgoing = outgoing.astype(jnp.bfloat16).reshape(dp_count, 1, block_rows, block_size)
    totals = one_axis_at_a_time(partial_value, DP)
    own_row = lax.dynamic_index_in_dim(select_full, owner_index, 0, keepdims=False)
    adam_sq = jnp.sum(own_row * totals.reshape(-1))
    left = left_root[0, 0]
    right = right_root[0, 0]
    rows_in = lax.all_to_all(outgoing, DP, split_axis=0, concat_axis=1, tiled=True)
    flat = rows_in.reshape(-1, block_size)
    product = jnp.dot(flat, right, preferred_element_type=jnp.float32).astype(jnp.bfloat16)
    mixed_rows = product.reshape(rows_in.shape)
    mixed = mixed_rows.reshape(block_size, block_size)
    shaped = jnp.dot(left, mixed, preferred_element_type=jnp.float32)
    shaped_sq = jnp.sum(shaped * shaped)
    factor = jnp.sqrt((adam_sq + NORM_EPS) / (shaped_sq + NORM_EPS))
    result = (shaped * factor).astype(jnp.bfloat16).reshape(1, dp_count, block_rows, block_size)
    back = lax.all_to_all(result, DP, split_axis=1, concat_axis=0, tiled=True)
    placed = jnp.einsum(
        "src,swk->rwck",
        select_half,
        back.reshape(dp_count, block_rows, block_size),
        preferred_element_type=jnp.float32,
    )
    return placed.astype(jnp.bfloat16).reshape(row_blocks, block_rows, half_cols)


def solution(mesh):
    split = Mesh(mesh.devices.reshape(4, 8, 4, mesh.shape["mp"]), ("dp_0", "dp_1", "dp_2", "mp"))
    return jax.shard_map(
        per_device,
        mesh=split,
        in_specs=(
            P(None, DP, "mp"),
            P(None, DP, "mp"),
            P("mp", DP, None, None),
            P("mp", DP, None, None),
            P(),
        ),
        out_specs=P(None, DP, "mp"),
        check_vma=False,
    )
```

profile of v0, /device:TPU:32, one launch (start us, length us, event | category | flops | bytes accessed | tf_op | source)
XLA Modules:
  0.0 170.4 jit_solution(4554805656612453106)
XLA Ops:
  0.0 0.0 copy-start
  0.0 0.8 fusion.41
  0.8 4.4 %fusion.18 = bf16[128,1,8,1024]{3,0,2,1:T(8,128)(2,1)S(1)} fusion(bf16[32,8,4,1024]{3,1,2,0:T(8,128)(2,1)} %bitcast.59, s32[32,4]{0,1:T(4,128)S(1)} %fusion.41), kind=kOutput, calls=%fused_computation.22 | convolution fusion | flops 269500416 | bytes 4194816 | tf_op jit(solution)/shard_map/src,rwck->swk/dot_general | solution.py:40
  5.2 2.5 %copy.28 = bf16[128,1,8,1024]{3,2,1,0:T(8,128)(2,1)} copy(bf16[128,1,8,1024]{3,0,2,1:T(8,128)(2,1)S(1)} %fusion.18) | data formatting | bytes 4194304 | tf_op jit(solution)/shard_map/reshape | solution.py:41
  7.7 0.0 copy-start.1
  7.7 15.6 %all-to-all-start = ((bf16[128,1,8,1024]{3,2,1,0:T(8,128)(2,1)}), bf16[128,1,8,1024]{3,2,1,0:T(8,128)(2,1)}, u32[]{:S(2)}, u32[]{:S(2)}) async-start(bf16[128,1,8,1024]{3,2,1,0:T(8,128)(2,1)} %copy.28), calls=%async_computation | async-start | bytes 4194304 | tf_op jit(solution)/shard_map/all_to_all | solution.py:47
  23.3 0.0 copy-done.1
  23.3 0.1 copy.29
  23.4 0.1 eq.28
  23.5 6.0 %fusion.4 = f32[32,4096]{1,0:T(8,128)S(1)} fusion(f32[32,8,4096]{2,1,0:T(8,128)} %param.6, bf16[32,8,4096]{2,1,0:T(8,128)(2,1)} %param.5), kind=kLoop, calls=%fused_computation.9 | loop fusion | flops 9306112 | bytes 6815744 | tf_op jit(solution)/shard_map/reduce_sum | solution.py:31
  29.5 0.4 reduce_sum.35
  29.9 0.1 reduce_sum.36
  30.0 0.1 copy.37
  30.1 11.2 %psum.21 = f32[32,4]{0,1:T(4,128)S(1)} all-reduce(f32[32,4]{0,1:T(4,128)S(1)} %copy.37), channel_id=1, replica_groups=mesh['dp_0'=4,'dp_1'=8,'dp_2'=4,'mp'=2] {'dp_0'}, use_global_device_ids=true, to_apply=%region_2.3 | all-reduce | flops 128 | bytes 1024 | tf_op jit(solution)/shard_map/psum | solution.py:17
  41.3 36.2 %psum.22 = f32[32,4]{0,1:T(4,128)S(1)} all-reduce(f32[32,4]{0,1:T(4,128)S(1)} %psum.21), channel_id=1, replica_groups=mesh['dp_0'=4,'dp_1'=8,'dp_2'=4,'mp'=2] {'dp_1'}, use_global_device_ids=true, to_apply=%region_3.4 | all-reduce | flops 128 | bytes 1024 | tf_op jit(solution)/shard_map/psum | solution.py:17
  77.5 0.1 copy.31
  77.6 0.1 reshape.37
  77.7 10.8 %psum.23 = f32[128]{0:T(128)S(1)} all-reduce(f32[128]{0:T(128)S(1)} %reshape.37), channel_id=1, replica_groups=mesh['dp_0'=4,'dp_1'=8,'dp_2'=4,'mp'=2] {'dp_2'}, use_global_device_ids=true, to_apply=%region_4.5 | all-reduce | flops 128 | bytes 1024 | tf_op jit(solution)/shard_map/psum | solution.py:17
  88.5 0.7 fusion.36
  89.9 0.0 all-to-all-done
  89.9 0.0 copy-done
  89.9 9.2 %multiply_reduce_fusion = (f32[]{:T(128)}, f32[1024,1024]{0,1:T(8,128)}) fusion(bf16[1,1,1024,1024]{3,2,1,0:T(8,128)(2,1)S(1)} %copy-done, bf16[128,1,8,1024]{3,2,1,0:T(8,128)(2,1)} %all-to-all-done, bf16[1,1,1024,1024]{3,2,1,0:T(8,128)(2,1)} %param.7), kind=kOutput, calls=%fused_computation.8 | convolution fusion | flops 4298113024 | bytes 10485764 | tf_op jit(solution)/shard_map/dot_general | solution.py:52
  99.9 2.8 %fusion.5 = bf16[1,128,8,1024]{3,2,0,1:T(8,128)(2,1)S(1)} fusion(f32[1024,1024]{0,1:T(8,128)} %get-tuple-element.6, f32[]{:T(128)S(6)} %sqrt.7), kind=kLoop, calls=%fused_computation.10 | loop fusion | flops 2097152 | bytes 6291460 | tf_op jit(solution)/shard_map/reshape | solution.py:55
  102.6 58.6 %all_to_all.8 = bf16[1,128,8,1024]{3,2,0,1:T(8,128)(2,1)S(1)} all-to-all(bf16[1,128,8,1024]{3,2,0,1:T(8,128)(2,1)S(1)} %fusion.5), channel_id=1, replica_groups=mesh['dp_0'=4,'dp_1'=8,'dp_2'=4,'mp'=2] {'dp_0','dp_1','dp_2'}, dimensions={1} | all-to-all | bytes 4194304 | tf_op jit(solution)/shard_map/all_to_all | solution.py:56
  161.2 1.7 %convert_bitcast_fusion = bf16[32,8,4,1024]{3,0,2,1:T(8,128)(2,1)S(1)} fusion(bf16[1,128,8,1024]{3,2,0,1:T(8,128)(2,1)S(1)} %all_to_all.8, s32[32,4]{0,1:T(4,128)S(1)} %fusion.41), kind=kOutput, calls=%fused_computation.20 | convolution fusion | flops 269500416 | bytes 4194816 | tf_op jit(solution)/shard_map/src,swk->rwck/dot_general | solution.py:57
  163.0 3.0 %copy.34 = bf16[32,8,4,1024]{3,2,1,0:T(4,128)(2,1)} copy(bf16[32,8,4,1024]{3,0,2,1:T(8,128)(2,1)S(1)} %convert_bitcast_fusion) | data formatting | bytes 4194304 | tf_op jit(solution)/shard_map/convert_element_type | solution.py:63
  165.9 4.5 %reshape.40 = bf16[32,8,4096]{2,1,0:T(8,128)(2,1)} reshape(bf16[32,8,4,1024]{3,2,1,0:T(4,128)(2,1)} %copy.34) | data formatting | bytes 4194304 | tf_op jit(solution)/shard_map/reshape | solution.py:63
  (1 shorter events, 0.0 us)
Async XLA Ops:
  0.0 89.9 %copy-start = (bf16[1,1,1024,1024]{3,2,1,0:T(8,128)(2,1)S(1)}, bf16[1,1,1024,1024]{3,2,1,0:T(8,128)(2,1)}, u32[]{:S(2)}) copy-start(bf16[1,1,1024,1024]{3,2,1,0:T(8,128)(2,1)} %param.8) | copy-start | bytes 6291460
  7.7 15.6 %copy-start.1 = (s32[2,32,4]{1,2,0:T(4,128)S(1)}, s32[2,32,4]{1,2,0:T(4,128)}, u32[]{:S(2)}) copy-start(s32[2,32,4]{1,2,0:T(4,128)} %param.9) | copy-start | bytes 3076
  7.7 82.2 %all-to-all-start = ((bf16[128,1,8,1024]{3,2,1,0:T(8,128)(2,1)}), bf16[128,1,8,1024]{3,2,1,0:T(8,128)(2,1)}, u32[]{:S(2)}, u32[]{:S(2)}) async-start(bf16[128,1,8,1024]{3,2,1,0:T(8,128)(2,1)} %copy.28), calls=%async_computation | async-start | bytes 4194304 | tf_op jit(solution)/shard_map/all_to_all | solution.py:47
where the time goes:
time: 171 us; the launch traced here: 170 us
  blocking collectives  117 us (68%)
  starting transfers between devices  15.6 us (9%)
  matrix products  15.3 us (9%)
  local copies, waits for them, and re-layouts  11.6 us (7%)
  other arithmetic  9.62 us (6%)
    all_to_all x1, blocking collectives, per_device(): back = lax.all_to_all(result, DP, split_axis=1, concat_axis=0, tiled=True)  58.6 us
    psum x3, blocking collectives, one_axis_at_a_time(): value = lax.psum(value, axis)  58.2 us
    all_to_all x1, starting transfers between devices, per_device(): lax.all_to_all(outgoing, DP, split_axis=0, concat_axis=1, tiled=True)  15.6 us
    dot_general x1, matrix products, per_device(): shaped = jnp.dot(left, mixed, preferred_element_type=jnp.float32)  9.24 us
    reduce_sum x2, other arithmetic, per_device(): jnp.sum((direction * direction).reshape(row_blocks, block_rows, col_block...  6.16 us
    reshape x1, local copies, waits for them, and re-layouts, per_device(): placed.astype(jnp.bfloat16).reshape(row_blocks, block_rows, half_cols)  4.45 us
    dot_general x1, matrix products, per_device(): jnp.einsum('src,rwck->swk', select_half, tiles, preferred_element_type=jn...  4.35 us
  transfers between devices with their start and end apart: 1, of which 0 were waited for; matrix products, arithmetic and copies ran while one was open for 5% of the time, Pallas kernels for 0%

commit v1 on v0

v1 whole, which is shorter than its diff:
```python
import functools

import jax
import jax.numpy as jnp
from jax import lax
from jax.experimental import pallas as pl
from jax.experimental.pallas import tpu as pltpu
from jax.sharding import Mesh
from jax.sharding import PartitionSpec as P

DP = ("dp_0", "dp_1", "dp_2")


BETA_TWO = 0.99
ADAM_EPS = 1e-08
NORM_EPS = 1e-06
MIB = 1 << 20


def gather_kernel(groups, table_ref, grad_ref, out_ref, held_ref, in_sem, out_sem):
    row_blocks = grad_ref.shape[0]
    block_size = out_ref.shape[-1]
    col_blocks = grad_ref.shape[2] // block_size
    group = row_blocks // groups
    base = lax.axis_index("mp") * (row_blocks * col_blocks)

    def load(g):
        rows = pl.ds(g * group, group)
        return pltpu.make_async_copy(grad_ref.at[rows], held_ref.at[rows], in_sem.at[g])

    for g in range(groups):
        load(g).start()
    for g in range(groups):
        load(g).wait()

        def one_row(row, carry):
            for col in range(col_blocks):
                slot = table_ref[base + row * col_blocks + col]
                pltpu.make_async_copy(
                    held_ref.at[row, :, pl.ds(col * block_size, block_size)], out_ref.at[slot], out_sem
                ).start()
            return carry

        lax.fori_loop(g * group, (g + 1) * group, one_row, 0)
    pltpu.make_async_copy(out_ref, out_ref, out_sem).wait()


def scatter_kernel(table_ref, back_ref, out_ref, sem):
    row_blocks = out_ref.shape[0]
    block_size = back_ref.shape[-1]
    col_blocks = out_ref.shape[2] // block_size
    base = lax.axis_index("mp") * (row_blocks * col_blocks)

    def one_row(row, carry):
        for col in range(col_blocks):
            slot = table_ref[base + row * col_blocks + col]
            pltpu.make_async_copy(
                back_ref.at[slot], out_ref.at[row, :, pl.ds(col * block_size, block_size)], sem
            ).start()
        return carry

    lax.fori_loop(0, row_blocks, one_row, 0)
    pltpu.make_async_copy(out_ref, out_ref, sem).wait()


def block_kernel(parts, tile, table_ref, *refs):
    part_refs = refs[:parts]
    rows_hbm, right_hbm, left_hbm, out_ref, rows_ref, right_ref, left_ref, mixed_ref, shaped_ref, sem = refs[parts:]
    block_size = right_hbm.shape[0]
    steps = block_size // tile

    def rows_load(i):
        rows = pl.ds(i * tile, tile)
        return pltpu.make_async_copy(rows_hbm.at[rows], rows_ref.at[rows], sem.at[i])

    def right_load(i):
        cols = pl.ds(i * tile, tile)
        return pltpu.make_async_copy(right_hbm.at[:, cols], right_ref.at[:, cols], sem.at[steps + i])

    left_load = pltpu.make_async_copy(left_hbm, left_ref, sem.at[2 * steps])
    right_load(0).start()
    for i in range(steps):
        rows_load(i).start()
    for i in range(1, steps):
        right_load(i).start()
    left_load.start()
    me = lax.axis_index(DP)
    totals = part_refs[0][...]
    for part_ref in part_refs[1:]:
        totals = totals + part_ref[...]
    adam_sq = jnp.sum(jnp.where(table_ref[...] == me, totals, 0.0))
    for j in range(steps):
        cols = pl.ds(j * tile, tile)
        right_load(j).wait()
        for i in range(steps):
            rows = pl.ds(i * tile, tile)
            if j == 0:
                rows_load(i).wait()
            mixed_ref[rows, cols] = jnp.dot(
                rows_ref[rows, :], right_ref[:, cols], preferred_element_type=jnp.float32
            ).astype(jnp.bfloat16)
    left_load.wait()
    squares = jnp.zeros((8, tile), jnp.float32)
    for i in range(steps):
        cols = pl.ds(i * tile, tile)
        shaped = jnp.dot(left_ref[...], mixed_ref[:, cols], preferred_element_type=jnp.float32)
        shaped_ref[:, cols] = shaped
        squares = squares + jnp.sum((shaped * shaped).reshape(block_size // 8, 8, tile), axis=0)
    shaped_sq = jnp.sum(squares)
    factor = jnp.sqrt(jnp.full((8, 128), adam_sq + NORM_EPS, jnp.float32) / (shaped_sq + NORM_EPS))
    scale = factor[0:1, 0:1]
    out_ref[...] = (shaped_ref[...] * scale).astype(jnp.bfloat16)


def per_device(grad, second_moment, left_root, right_root, owner_slot):
    row_blocks, block_rows, half_cols = grad.shape
    block_size = left_root.shape[-1]
    col_blocks = half_cols // block_size
    blocks = row_blocks * col_blocks
    dp_count = lax.axis_size(DP)
    mp_index = lax.axis_index("mp")
    table = owner_slot.reshape(-1)
    vmem = pl.BlockSpec(memory_space=pltpu.VMEM)
    hbm = pl.BlockSpec(memory_space=pltpu.HBM)
    smem = pl.BlockSpec(memory_space=pltpu.SMEM)
    square = jax.ShapeDtypeStruct((block_size, block_size), jnp.bfloat16)
    groups = 4

    def in_hbm(value):
        return pltpu.with_memory_space_constraint(value, pltpu.HBM)

    outgoing = pl.pallas_call(
        functools.partial(gather_kernel, groups),
        out_shape=jax.ShapeDtypeStruct((dp_count, block_rows, block_size), jnp.bfloat16),
        in_specs=[smem, hbm],
        out_specs=hbm,
        scratch_shapes=[
            pltpu.VMEM(grad.shape, jnp.bfloat16),
            pltpu.SemaphoreType.DMA((groups,)),
            pltpu.SemaphoreType.DMA,
        ],
        name="gather_rows",
    )(table, grad)
    rows_in = lax.all_to_all(outgoing, DP, split_axis=0, concat_axis=0, tiled=True)

    widened = grad.astype(jnp.float32)
    moment_new = BETA_TWO * second_moment + (1.0 - BETA_TWO) * widened * widened
    direction = widened / (jnp.sqrt(moment_new) + ADAM_EPS)
    partial_value = jnp.sum(
        (direction * direction).reshape(row_blocks, block_rows, col_blocks, block_size), axis=(1, 3)
    ).reshape(1, blocks)
    plane = lax.psum(lax.psum(partial_value, "dp_0"), "dp_2")
    depth = lax.axis_size("dp_1")
    parts = [plane]
    for step in range(1, depth):
        ring = [(i, (i + step) % depth) for i in range(depth)]
        parts.append(lax.ppermute(plane, "dp_1", ring))
    half_table = lax.dynamic_index_in_dim(owner_slot, mp_index, 0, keepdims=False).reshape(1, blocks)

    tile = block_size // 4
    result = pl.pallas_call(
        functools.partial(block_kernel, depth, tile),
        out_shape=square,
        in_specs=[vmem] * (depth + 1) + [hbm] * 3,
        out_specs=vmem,
        scratch_shapes=[
            pltpu.VMEM((block_size, block_size), jnp.bfloat16),
            pltpu.VMEM((block_size, block_size), jnp.bfloat16),
            pltpu.VMEM((block_size, block_size), jnp.bfloat16),
            pltpu.VMEM((block_size, block_size), jnp.bfloat16),
            pltpu.VMEM((block_size, block_size), jnp.float32),
            pltpu.SemaphoreType.DMA((2 * (block_size // tile) + 1,)),
        ],
        compiler_params=pltpu.CompilerParams(vmem_limit_bytes=24 * MIB),
        name="own_block",
        cost_estimate=pl.CostEstimate(
            flops=4 * block_size**3, bytes_accessed=8 * block_size**2, transcendentals=0
        ),
    )(half_table, *parts, in_hbm(rows_in.reshape(block_size, block_size)), in_hbm(right_root[0, 0]), in_hbm(left_root[0, 0]))

    back = lax.all_to_all(
        result.reshape(dp_count, block_rows, block_size), DP, split_axis=0, concat_axis=0, tiled=True
    )
    return pl.pallas_call(
        scatter_kernel,
        out_shape=jax.ShapeDtypeStruct(grad.shape, jnp.bfloat16),
        in_specs=[smem, vmem],
        out_specs=hbm,
        scratch_shapes=[pltpu.SemaphoreType.DMA],
        compiler_params=pltpu.CompilerParams(vmem_limit_bytes=8 * MIB),
        name="scatter_rows",
    )(table, back)


def solution(mesh):
    split = Mesh(mesh.devices.reshape(4, 8, 4, mesh.shape["mp"]), ("dp_0", "dp_1", "dp_2", "mp"))
    return jax.shard_map(
        per_device,
        mesh=split,
        in_specs=(
            P(None, DP, "mp"),
            P(None, DP, "mp"),
            P("mp", DP, None, None),
            P("mp", DP, None, None),
            P(),
        ),
        out_specs=P(None, DP, "mp"),
        check_vma=False,
    )
```

time: 171 us -> 145 us (0.85)
  blocking collectives: 117 us -> 83.9 us
  starting transfers between devices: 15.6 us -> 33.4 us
  matrix products: 15.3 us -> 0 us
  Pallas kernels: 0 us -> 13.1 us
  local copies, waits for them, and re-layouts: 11.6 us -> 2.12 us
  waiting for transfers between devices: 0.01 us -> 6.5 us
  other arithmetic: 9.62 us -> 5.48 us
    psum x3 -> x2, blocking collectives: 58.2 us -> 21.5 us  [per_device(): plane = lax.psum(lax.psum(partial_value, 'dp_0'), 'dp_2')]
    ppermute x0 -> x7, starting transfers between devices: none -> 17.9 us  [per_device(): parts.append(lax.ppermute(plane, 'dp_1', ring))]
    dot_general x3 -> x0, matrix products: 15.3 us -> none  [the longest x1 9.24 us: per_device(): shaped = jnp.dot(left, mixed, preferred_element_type=jnp.float32)]
    pallas_call x0 -> x3, Pallas kernels: none -> 13.1 us  [the longest x1 8.1 us: per_device(): pl.pallas_call(functools.partial(block_kernel, depth, tile), out_shape=sq...]
    ppermute x0 -> x7, waiting for transfers between devices: none -> 6.5 us  [per_device(): parts.append(lax.ppermute(plane, 'dp_1', ring))]
    reshape x3, local copies, waits for them, and re-layouts: 7.03 us -> 0.89 us  [the longest x1 0.69 us: per_device(): table = owner_slot.reshape(-1)]
    all_to_all x1, blocking collectives: 58.6 us -> 62.4 us  [per_device(): lax.all_to_all(result.reshape(dp_count, block_rows, block_size), DP, spli...]
    convert_element_type x1 -> x0, local copies, waits for them, and re-layouts: 2.97 us -> none  [per_device(): placed.astype(jnp.bfloat16).reshape(row_blocks, block_rows, half_cols)]
  transfers between devices with their start and end apart: 1 -> 8, of which waited for: 0 -> 2; matrix products, arithmetic and copies ran while one was open for 5% -> 4% of each run, Pallas kernels for 0% -> 0%
where the time goes in v1:
time: 145 us
  blocking collectives  83.9 us (58%)
  starting transfers between devices  33.4 us (23%)
  Pallas kernels  13.1 us (9%)
  waiting for transfers between devices  6.5 us (4%)
  other arithmetic  5.48 us (4%)
  local copies, waits for them, and re-layouts  2.12 us (1%)
    all_to_all x1, blocking collectives, per_device(): lax.all_to_all(result.reshape(dp_count, block_rows, block_size), DP, spli...  62.4 us
    psum x2, blocking collectives, per_device(): plane = lax.psum(lax.psum(partial_value, 'dp_0'), 'dp_2')  21.5 us
    ppermute x7, starting transfers between devices, per_device(): parts.append(lax.ppermute(plane, 'dp_1', ring))  17.9 us
    all_to_all x1, starting transfers between devices, per_device(): lax.all_to_all(outgoing, DP, split_axis=0, concat_axis=0, tiled=True)  15.5 us
    pallas_call x1, Pallas kernels, per_device(): pl.pallas_call(functools.partial(block_kernel, depth, tile), out_shape=sq...  8.1 us
    ppermute x7, waiting for transfers between devices, per_device(): parts.append(lax.ppermute(plane, 'dp_1', ring))  6.5 us
    reduce_sum x2, other arithmetic, per_device(): jnp.sum((direction * direction).reshape(row_blocks, block_rows, col_block...  5.48 us
    pallas_call x1, Pallas kernels, per_device(): pl.pallas_call(functools.partial(gather_kernel, groups), out_shape=jax.Sh...  3.18 us
  transfers between devices with their start and end apart: 8, of which 2 were waited for; matrix products, arithmetic and copies ran while one was open for 4% of the time, Pallas kernels for 0%

profile of v1, /device:TPU:32, one launch (start us, length us, event | category | flops | bytes accessed | tf_op | source)
XLA Modules:
  0.0 144.8 jit_solution(9801527892393338193)
XLA Ops:
  0.0 0.8 copy.12
  0.8 0.7 reshape.18.table_ref
  1.5 0.0 copy-start.1
  1.5 3.2 %gather_rows.1 = bf16[128,8,1024]{2,1,0:T(8,128)(2,1)} custom-call(s32[256]{0:T(256)} %reshape.18.table_ref, bf16[32,8,4096]{2,1,0:T(8,128)(2,1)} %grad_ref.1), custom_call_target="tpu_custom_call" | custom-call | tf_op jit(solution)/shard_map/gather_rows/pallas_call | solution.py:132
  4.6 15.5 %all-to-all-start = ((bf16[128,8,1024]{2,1,0:T(8,128)(2,1)}), bf16[128,8,1024]{2,1,0:T(8,128)(2,1)}, u32[]{:S(2)}, u32[]{:S(2)}) async-start(bf16[128,8,1024]{2,1,0:T(8,128)(2,1)} %gather_rows.1), calls=%async_computation | async-start | bytes 4194304 | tf_op jit(solution)/shard_map/all_to_all | solution.py:144
  20.1 0.0 copy-done.1
  20.1 0.0 copy-start.2
  20.1 5.3 %fusion.4 = f32[32,4096]{1,0:T(8,128)S(1)} fusion(f32[32,8,4096]{2,1,0:T(8,128)} %param.6, bf16[32,8,4096]{2,1,0:T(8,128)(2,1)S(1)} %copy-done.1), kind=kLoop, calls=%fused_computation.6 | loop fusion | flops 9306112 | bytes 6815744 | tf_op jit(solution)/shard_map/reduce_sum | solution.py:149
  25.5 0.4 reduce_sum.14
  25.8 0.1 reduce_sum.18
  26.0 0.1 reshape.20
  26.1 11.6 %psum.14 = f32[1,128]{1,0:T(1,128)S(1)} all-reduce(f32[1,128]{1,0:T(1,128)S(1)} %reshape.20), channel_id=1, replica_groups=mesh['dp_0'=4,'dp_1'=8,'dp_2'=4,'mp'=2] {'dp_0'}, use_global_device_ids=true, to_apply=%region_2.0 | all-reduce | flops 128 | bytes 1024 | tf_op jit(solution)/shard_map/psum | solution.py:152
  37.7 9.9 %psum.15.refs_0_ = f32[1,128]{1,0:T(1,128)S(1)} all-reduce(f32[1,128]{1,0:T(1,128)S(1)} %psum.14), channel_id=1, replica_groups=mesh['dp_0'=4,'dp_1'=8,'dp_2'=4,'mp'=2] {'dp_2'}, use_global_device_ids=true, to_apply=%region_3.4 | all-reduce | flops 128 | bytes 1024 | tf_op jit(solution)/shard_map/psum | solution.py:152
  47.6 0.5 collective-permute-start.6
  48.1 3.7 %collective-permute-start.5 = (f32[1,128]{1,0:T(1,128)S(1)}, f32[1,128]{1,0:T(1,128)S(1)}, u32[]{:S(2)}, u32[]{:S(2)}) collective-permute-start(f32[1,128]{1,0:T(1,128)S(1)} %psum.15.refs_0_), channel_id=1, source_target_pairs={{0,48},{8,56},{16,0},{24,8},{32,16},{40,24},{48,32},{56,40},{1,49}... | collective-permute-start | bytes 1544 | tf_op jit(solution)/shard_map/ppermute | solution.py:157
  51.8 3.1 %collective-permute-start.4 = (f32[1,128]{1,0:T(1,128)S(1)}, f32[1,128]{1,0:T(1,128)S(1)}, u32[]{:S(2)}, u32[]{:S(2)}) collective-permute-start(f32[1,128]{1,0:T(1,128)S(1)} %psum.15.refs_0_), channel_id=1, source_target_pairs={{0,40},{8,48},{16,56},{24,0},{32,8},{40,16},{48,24},{56,32},{1,41}... | collective-permute-start | bytes 1544 | tf_op jit(solution)/shard_map/ppermute | solution.py:157
  54.9 1.9 %collective-permute-start.3 = (f32[1,128]{1,0:T(1,128)S(1)}, f32[1,128]{1,0:T(1,128)S(1)}, u32[]{:S(2)}, u32[]{:S(2)}) collective-permute-start(f32[1,128]{1,0:T(1,128)S(1)} %psum.15.refs_0_), channel_id=1, source_target_pairs={{0,32},{8,40},{16,48},{24,56},{32,0},{40,8},{48,16},{56,24},{1,33}... | collective-permute-start | bytes 1544 | tf_op jit(solution)/shard_map/ppermute | solution.py:157
  56.9 2.6 %collective-permute-start.2 = (f32[1,128]{1,0:T(1,128)S(1)}, f32[1,128]{1,0:T(1,128)S(1)}, u32[]{:S(2)}, u32[]{:S(2)}) collective-permute-start(f32[1,128]{1,0:T(1,128)S(1)} %psum.15.refs_0_), channel_id=1, source_target_pairs={{0,24},{8,32},{16,40},{24,48},{32,56},{40,0},{48,8},{56,16},{1,25}... | collective-permute-start | bytes 1544 | tf_op jit(solution)/shard_map/ppermute | solution.py:157
  59.5 4.3 %collective-permute-done.6.refs_7_ = f32[1,128]{1,0:T(1,128)S(1)} collective-permute-done((f32[1,128]{1,0:T(1,128)S(1)}, f32[1,128]{1,0:T(1,128)S(1)}, u32[]{:S(2)}, u32[]{:S(2)}) %collective-permute-start.6) | collective-permute-done | bytes 544 | tf_op jit(solution)/shard_map/ppermute | solution.py:157
  63.8 4.9 %collective-permute-start.1 = (f32[1,128]{1,0:T(1,128)S(1)}, f32[1,128]{1,0:T(1,128)S(1)}, u32[]{:S(2)}, u32[]{:S(2)}) collective-permute-start(f32[1,128]{1,0:T(1,128)S(1)} %psum.15.refs_0_), channel_id=1, source_target_pairs={{0,16},{8,24},{16,32},{24,40},{32,48},{40,56},{48,0},{56,8},{1,17}... | collective-permute-start | bytes 1544 | tf_op jit(solution)/shard_map/ppermute | solution.py:157
  68.6 0.0 collective-permute-done.5.refs_6_
  68.6 1.1 collective-permute-start
  69.8 0.0 copy-done.2
  69.8 0.1 copy.13
  69.9 0.1 reshape.19.table_ref
  70.0 0.0 collective-permute-done.4.refs_5_
  70.0 0.0 collective-permute-done.3.refs_4_
  70.0 0.0 collective-permute-done.2.refs_3_
  70.0 0.0 collective-permute-done.1.refs_2_
  70.0 2.2 %collective-permute-done.refs_1_ = f32[1,128]{1,0:T(1,128)S(1)} collective-permute-done((f32[1,128]{1,0:T(1,128)S(1)}, f32[1,128]{1,0:T(1,128)S(1)}, u32[]{:S(2)}, u32[]{:S(2)}) %collective-permute-start) | collective-permute-done | bytes 544 | tf_op jit(solution)/shard_map/ppermute | solution.py:157
  72.2 0.0 all-to-all-done
  72.2 8.1 %own_block.1 = bf16[1024,1024]{1,0:T(8,128)(2,1)S(1)} custom-call(s32[1,128]{1,0:T(1,128)S(1)} %reshape.19.table_ref, f32[1,128]{1,0:T(1,128)S(1)} %psum.15.refs_0_, f32[1,128]{1,0:T(1,128)S(1)} %collective-permute-done.refs_1_, f32[1,128]{1,0:T(1,128)S(1)} %collective-permute-done.1.refs_2_, f32[1,128]{1,0:T(1,128)S(1)} %collective-permute-done.2.refs_3_, ...), custom_call_target="tpu_custom_call" | custom-call | flops 4294967296 | bytes 8388608 | tf_op jit(solution)/shard_map/own_block/pallas_call | solution.py:161
  80.3 0.0 copy-start
  80.3 62.4 %all_to_all.10.back_ref = bf16[128,8,1024]{2,1,0:T(8,128)(2,1)S(1)} all-to-all(bf16[128,8,1024]{2,1,0:T(8,128)(2,1)S(1)} %bitcast.4), channel_id=1, replica_groups=mesh['dp_0'=4,'dp_1'=8,'dp_2'=4,'mp'=2] {'dp_0','dp_1','dp_2'}, dimensions={0} | all-to-all | bytes 4194304 | tf_op jit(solution)/shard_map/all_to_all | solution.py:181
  142.8 0.0 copy-done
  142.8 1.8 %scatter_rows.1 = bf16[32,8,4096]{2,1,0:T(8,128)(2,1)} custom-call(s32[256]{0:T(256)S(1)} %copy-done, bf16[128,8,1024]{2,1,0:T(8,128)(2,1)S(1)} %all_to_all.10.back_ref), custom_call_target="tpu_custom_call" | custom-call | tf_op jit(solution)/shard_map/scatter_rows/pallas_call | solution.py:184
  (1 shorter events, 0.0 us)
Async XLA Ops:
  1.5 18.7 %copy-start.1 = (bf16[32,8,4096]{2,1,0:T(8,128)(2,1)S(1)}, bf16[32,8,4096]{2,1,0:T(8,128)(2,1)}, u32[]{:S(2)}) copy-start(bf16[32,8,4096]{2,1,0:T(8,128)(2,1)} %grad_ref.1) | copy-start | bytes 6291460
  4.6 67.6 %all-to-all-start = ((bf16[128,8,1024]{2,1,0:T(8,128)(2,1)}), bf16[128,8,1024]{2,1,0:T(8,128)(2,1)}, u32[]{:S(2)}, u32[]{:S(2)}) async-start(bf16[128,8,1024]{2,1,0:T(8,128)(2,1)} %gather_rows.1), calls=%async_computation | async-start | bytes 4194304 | tf_op jit(solution)/shard_map/all_to_all | solution.py:144
  20.1 49.6 %copy-start.2 = (s32[2,32,4]{1,2,0:T(4,128)S(1)}, s32[2,32,4]{1,2,0:T(4,128)}, u32[]{:S(2)}) copy-start(s32[2,32,4]{1,2,0:T(4,128)} %param.9) | copy-start | bytes 3076
  47.6 16.2 %collective-permute-start.6 = (f32[1,128]{1,0:T(1,128)S(1)}, f32[1,128]{1,0:T(1,128)S(1)}, u32[]{:S(2)}, u32[]{:S(2)}) collective-permute-start(f32[1,128]{1,0:T(1,128)S(1)} %psum.15.refs_0_), channel_id=1, source_target_pairs={{0,56},{8,0},{16,8},{24,16},{32,24},{40,32},{48,40},{56,48},{1,57}... | collective-permute-start | bytes 1544 | tf_op jit(solution)/shard_map/ppermute | solution.py:157
  48.1 20.5 %collective-permute-start.5 = (f32[1,128]{1,0:T(1,128)S(1)}, f32[1,128]{1,0:T(1,128)S(1)}, u32[]{:S(2)}, u32[]{:S(2)}) collective-permute-start(f32[1,128]{1,0:T(1,128)S(1)} %psum.15.refs_0_), channel_id=1, source_target_pairs={{0,48},{8,56},{16,0},{24,8},{32,16},{40,24},{48,32},{56,40},{1,49}... | collective-permute-start | bytes 1544 | tf_op jit(solution)/shard_map/ppermute | solution.py:157
  51.8 18.1 %collective-permute-start.4 = (f32[1,128]{1,0:T(1,128)S(1)}, f32[1,128]{1,0:T(1,128)S(1)}, u32[]{:S(2)}, u32[]{:S(2)}) collective-permute-start(f32[1,128]{1,0:T(1,128)S(1)} %psum.15.refs_0_), channel_id=1, source_target_pairs={{0,40},{8,48},{16,56},{24,0},{32,8},{40,16},{48,24},{56,32},{1,41}... | collective-permute-start | bytes 1544 | tf_op jit(solution)/shard_map/ppermute | solution.py:157
  54.9 15.0 %collective-permute-start.3 = (f32[1,128]{1,0:T(1,128)S(1)}, f32[1,128]{1,0:T(1,128)S(1)}, u32[]{:S(2)}, u32[]{:S(2)}) collective-permute-start(f32[1,128]{1,0:T(1,128)S(1)} %psum.15.refs_0_), channel_id=1, source_target_pairs={{0,32},{8,40},{16,48},{24,56},{32,0},{40,8},{48,16},{56,24},{1,33}... | collective-permute-start | bytes 1544 | tf_op jit(solution)/shard_map/ppermute | solution.py:157
  56.9 13.1 %collective-permute-start.2 = (f32[1,128]{1,0:T(1,128)S(1)}, f32[1,128]{1,0:T(1,128)S(1)}, u32[]{:S(2)}, u32[]{:S(2)}) collective-permute-start(f32[1,128]{1,0:T(1,128)S(1)} %psum.15.refs_0_), channel_id=1, source_target_pairs={{0,24},{8,32},{16,40},{24,48},{32,56},{40,0},{48,8},{56,16},{1,25}... | collective-permute-start | bytes 1544 | tf_op jit(solution)/shard_map/ppermute | solution.py:157
  63.8 6.2 %collective-permute-start.1 = (f32[1,128]{1,0:T(1,128)S(1)}, f32[1,128]{1,0:T(1,128)S(1)}, u32[]{:S(2)}, u32[]{:S(2)}) collective-permute-start(f32[1,128]{1,0:T(1,128)S(1)} %psum.15.refs_0_), channel_id=1, source_target_pairs={{0,16},{8,24},{16,32},{24,40},{32,48},{40,56},{48,0},{56,8},{1,17}... | collective-permute-start | bytes 1544 | tf_op jit(solution)/shard_map/ppermute | solution.py:157
  68.6 3.6 %collective-permute-start = (f32[1,128]{1,0:T(1,128)S(1)}, f32[1,128]{1,0:T(1,128)S(1)}, u32[]{:S(2)}, u32[]{:S(2)}) collective-permute-start(f32[1,128]{1,0:T(1,128)S(1)} %psum.15.refs_0_), channel_id=1, source_target_pairs={{0,8},{8,16},{16,24},{24,32},{32,40},{40,48},{48,56},{56,0},{1,9},... | collective-permute-start | bytes 1544 | tf_op jit(solution)/shard_map/ppermute | solution.py:157
  80.3 62.4 %copy-start = (s32[256]{0:T(256)S(1)}, s32[256]{0:T(256)}, u32[]{:S(2)}) copy-start(s32[256]{0:T(256)} %reshape.18.table_ref) | copy-start | bytes 3076

commit v2 on v1

v2 whole, which is shorter than its diff:
```python
import functools

import jax
import jax.numpy as jnp
from jax import lax
from jax.experimental import pallas as pl
from jax.experimental.pallas import tpu as pltpu
from jax.sharding import Mesh
from jax.sharding import PartitionSpec as P

DP = ("dp_0", "dp_1", "dp_2")


BETA_TWO = 0.99
ADAM_EPS = 1e-08
NORM_EPS = 1e-06
MIB = 1 << 20
VMEM = pl.BlockSpec(memory_space=pltpu.VMEM)
HBM = pl.BlockSpec(memory_space=pltpu.HBM)
SMEM = pl.BlockSpec(memory_space=pltpu.SMEM)


def in_hbm(value):
    return pltpu.with_memory_space_constraint(value, pltpu.HBM)


def gather_kernel(groups, half, table_ref, grad_ref, out_ref, held_ref, in_sem, out_sem):
    row_blocks = grad_ref.shape[0]
    block_size = out_ref.shape[-1]
    col_blocks = grad_ref.shape[2] // block_size
    group = row_blocks // groups

    def load(g):
        rows = pl.ds(g * group, group)
        return pltpu.make_async_copy(grad_ref.at[rows], held_ref.at[rows], in_sem.at[g])

    for g in range(groups):
        load(g).start()
    for g in range(groups):
        load(g).wait()

        def one_row(row, carry):
            for col in range(col_blocks):
                pltpu.make_async_copy(
                    held_ref.at[row, :, pl.ds(col * block_size, block_size)],
                    out_ref.at[table_ref[half, col, row]],
                    out_sem,
                ).start()
            return carry

        lax.fori_loop(g * group, (g + 1) * group, one_row, 0)
    pltpu.make_async_copy(out_ref, out_ref, out_sem).wait()


def gather_rows(table, grad, half, slots, block_size):
    groups = 4
    return pl.pallas_call(
        functools.partial(gather_kernel, groups, half),
        out_shape=pltpu.HBM((slots, grad.shape[1], block_size), jnp.bfloat16),
        in_specs=[SMEM, HBM],
        out_specs=HBM,
        scratch_shapes=[
            pltpu.VMEM(grad.shape, jnp.bfloat16),
            pltpu.SemaphoreType.DMA((groups,)),
            pltpu.SemaphoreType.DMA,
        ],
        name="gather_rows",
    )(table, grad)


def scatter_kernel(half, table_ref, back_ref, out_ref, sem):
    row_blocks = out_ref.shape[0]
    block_size = back_ref.shape[-1]
    col_blocks = out_ref.shape[2] // block_size

    def one_row(row, carry):
        for col in range(col_blocks):
            pltpu.make_async_copy(
                back_ref.at[table_ref[half, col, row]],
                out_ref.at[row, :, pl.ds(col * block_size, block_size)],
                sem,
            ).start()
        return carry

    lax.fori_loop(0, row_blocks, one_row, 0)
    pltpu.make_async_copy(out_ref, out_ref, sem).wait()


def scaled_scatter_kernel(parts, half, table_ref, *refs):
    part_refs = refs[:parts]
    back_ref, out_ref, norm_ref, held_ref, sem = refs[parts:]
    row_blocks = out_ref.shape[0]
    block_size = back_ref.shape[-1]
    col_blocks = out_ref.shape[2] // block_size
    blocks = row_blocks * col_blocks
    totals = part_refs[0][...]
    for part_ref in part_refs[1:]:
        totals = totals + part_ref[...]
    norms = jnp.sqrt(totals + NORM_EPS)
    norm_ref[...] = jnp.transpose(jnp.broadcast_to(norms, (blocks, blocks)))

    def one_row(row, carry):
        for col in range(col_blocks):
            slot = table_ref[half, col, row]
            norm = norm_ref[pl.ds(row * col_blocks + col, 1), :]
            norm = jnp.concatenate([norm] * (block_size // blocks), axis=1)
            rows = back_ref[slot].astype(jnp.float32) * norm
            held_ref[row, :, pl.ds(col * block_size, block_size)] = rows.astype(jnp.bfloat16)
        pltpu.make_async_copy(held_ref.at[row], out_ref.at[row], sem).start()
        return carry

    lax.fori_loop(0, row_blocks, one_row, 0)
    pltpu.make_async_copy(out_ref, out_ref, sem).wait()


def scatter_rows(table, back, half, like, parts=None):
    out_shape = pltpu.HBM(like.shape, jnp.bfloat16)
    params = pltpu.CompilerParams(vmem_limit_bytes=8 * MIB)
    if parts is None:
        return pl.pallas_call(
            functools.partial(scatter_kernel, half),
            out_shape=out_shape,
            in_specs=[SMEM, VMEM],
            out_specs=HBM,
            scratch_shapes=[pltpu.SemaphoreType.DMA],
            compiler_params=params,
            name="scatter_rows",
        )(table, back)
    blocks = parts[0].shape[1]
    return pl.pallas_call(
        functools.partial(scaled_scatter_kernel, len(parts), half),
        out_shape=out_shape,
        in_specs=[SMEM] + [VMEM] * (len(parts) + 1),
        out_specs=HBM,
        scratch_shapes=[
            pltpu.VMEM((blocks, blocks), jnp.float32),
            pltpu.VMEM(like.shape, jnp.bfloat16),
            pltpu.SemaphoreType.DMA,
        ],
        compiler_params=params,
        name="scaled_scatter_rows",
    )(table, *parts, back)


def block_kernel(parts, tile, *refs):
    if parts > 0:
        table_ref, part_refs, refs = refs[0], refs[1 : 1 + parts], refs[1 + parts :]
    rows_hbm, right_hbm, left_hbm, out_hbm, rows_ref, right_ref, left_ref, mixed_ref, shaped_ref, out_ref, sem = refs
    block_size = right_hbm.shape[0]
    steps = block_size // tile

    def rows_load(i):
        rows = pl.ds(i * tile, tile)
        return pltpu.make_async_copy(rows_hbm.at[rows], rows_ref.at[rows], sem.at[i])

    def right_load(i):
        cols = pl.ds(i * tile, tile)
        return pltpu.make_async_copy(right_hbm.at[:, cols], right_ref.at[:, cols], sem.at[steps + i])

    def store(i):
        rows = pl.ds(i * tile, tile)
        return pltpu.make_async_copy(out_ref.at[rows], out_hbm.at[rows], sem.at[i])

    left_load = pltpu.make_async_copy(left_hbm, left_ref, sem.at[2 * steps])
    right_load(0).start()
    for i in range(steps):
        rows_load(i).start()
    for i in range(1, steps):
        right_load(i).start()
    left_load.start()
    adam_sq = None
    if parts > 0:
        totals = part_refs[0][...]
        for part_ref in part_refs[1:]:
            totals = totals + part_ref[...]
        adam_sq = jnp.sum(jnp.where(table_ref[...] == lax.axis_index(DP), totals, 0.0))
    for i in range(steps):
        rows_load(i).wait()

    def mix(j, carry):
        cols = pl.ds(pl.multiple_of(j * tile, tile), tile)
        right_load(j).wait()
        mixed_ref[:, cols] = jnp.dot(
            rows_ref[...], right_ref[:, cols], preferred_element_type=jnp.float32
        ).astype(jnp.bfloat16)
        return carry

    lax.fori_loop(0, steps, mix, 0)
    left_load.wait()

    def shape(j, squares):
        cols = pl.ds(pl.multiple_of(j * tile, tile), tile)
        shaped = jnp.dot(left_ref[...], mixed_ref[:, cols], preferred_element_type=jnp.float32)
        shaped_ref[:, cols] = shaped
        return squares + jnp.sum((shaped * shaped).reshape(block_size // 8, 8, tile), axis=0)

    squares = lax.fori_loop(0, steps, shape, jnp.zeros((8, tile), jnp.float32))
    shaped_sq = jnp.full((8, 128), jnp.sum(squares), jnp.float32)
    if parts > 0:
        factor = jnp.sqrt((adam_sq + NORM_EPS) / (shaped_sq + NORM_EPS))
    else:
        factor = 1.0 / jnp.sqrt(shaped_sq + NORM_EPS)
    scale = factor[0:1, 0:1]

    def finish(i, carry):
        rows = pl.ds(pl.multiple_of(i * tile, tile), tile)
        out_ref[rows, :] = (shaped_ref[rows, :] * scale).astype(jnp.bfloat16)
        store(i).start()
        return carry

    lax.fori_loop(0, steps, finish, 0)
    for i in range(steps):
        store(i).wait()


def own_block(rows_in, right, left, table=None, parts=()):
    block_size = right.shape[0]
    tile = block_size // 4
    square = pltpu.VMEM((block_size, block_size), jnp.bfloat16)
    small = () if table is None else (table, *parts)
    return pl.pallas_call(
        functools.partial(block_kernel, len(parts), tile),
        out_shape=pltpu.HBM((block_size, block_size), jnp.bfloat16),
        in_specs=[VMEM] * len(small) + [HBM] * 3,
        out_specs=HBM,
        scratch_shapes=[
            square,
            square,
            square,
            square,
            pltpu.VMEM((block_size, block_size), jnp.float32),
            square,
            pltpu.SemaphoreType.DMA((2 * (block_size // tile) + 1,)),
        ],
        compiler_params=pltpu.CompilerParams(vmem_limit_bytes=32 * MIB),
        name="own_block",
        cost_estimate=pl.CostEstimate(
            flops=4 * block_size**3, bytes_accessed=8 * block_size**2, transcendentals=0
        ),
    )(*small, in_hbm(rows_in), in_hbm(right), in_hbm(left))


def exchange(value):
    return lax.all_to_all(value, DP, split_axis=0, concat_axis=0, tiled=True)


def plane_sums(grad, second_moment, block_size):
    row_blocks, block_rows, half_cols = grad.shape
    col_blocks = half_cols // block_size
    widened = grad.astype(jnp.float32)
    moment_new = BETA_TWO * second_moment + (1.0 - BETA_TWO) * widened * widened
    direction = widened / (jnp.sqrt(moment_new) + ADAM_EPS)
    partial_value = jnp.sum(
        (direction * direction).reshape(row_blocks, block_rows, col_blocks, block_size), axis=(1, 3)
    ).reshape(1, row_blocks * col_blocks)
    return lax.psum(lax.psum(partial_value, "dp_0"), "dp_2")


def all_planes(plane):
    depth = lax.axis_size("dp_1")
    parts = [plane]
    for step in range(1, depth):
        ring = [(i, (i + step) % depth) for i in range(depth)]
        parts.append(lax.ppermute(plane, "dp_1", ring))
    return parts


def first_core(grad, second_moment, left, right, table):
    block_size = left.shape[0]
    slots = lax.axis_size(DP)
    outgoing = gather_rows(table, grad, 0, slots, block_size)
    rows_in = exchange(outgoing)
    plane = plane_sums(grad, second_moment, block_size)
    result = own_block(rows_in.reshape(block_size, block_size), right, left)
    plane, result = lax.optimization_barrier((plane, result))
    back = exchange(result.reshape(outgoing.shape))
    return scatter_rows(table, back, 0, grad, all_planes(plane))


def second_core(grad, second_moment, left, right, table):
    block_size = left.shape[0]
    slots = lax.axis_size(DP)
    outgoing = gather_rows(table, grad, 1, slots, block_size)
    plane = plane_sums(grad, second_moment, block_size)
    plane, outgoing = lax.optimization_barrier((plane, outgoing))
    rows_in = exchange(outgoing)
    own_table = jnp.transpose(table[1]).reshape(1, -1)
    result = own_block(
        rows_in.reshape(block_size, block_size), right, left, own_table, all_planes(plane)
    )
    back = exchange(result.reshape(outgoing.shape))
    return scatter_rows(table, back, 1, grad)


def per_device(grad, second_moment, left_root, right_root, owner_slot):
    table = jnp.transpose(owner_slot, (0, 2, 1))
    return lax.cond(
        lax.axis_index("mp") == 0,
        first_core,
        second_core,
        grad,
        second_moment,
        left_root[0, 0],
        right_root[0, 0],
        table,
    )


def solution(mesh):
    split = Mesh(mesh.devices.reshape(4, 8, 4, mesh.shape["mp"]), ("dp_0", "dp_1", "dp_2", "mp"))
    return jax.shard_map(
        per_device,
        mesh=split,
        in_specs=(
            P(None, DP, "mp"),
            P(None, DP, "mp"),
            P("mp", DP, None, None),
            P("mp", DP, None, None),
            P(),
        ),
        out_specs=P(None, DP, "mp"),
        check_vma=False,
    )
```

time: 145 us -> 129 us (0.89)
  the two profiles are of different devices: /device:TPU:32 before, /device:TPU:1 now
where the time goes in v2:
time: 129 us; the launch traced here: 128 us
  blocking collectives  60.7 us (47%)
  starting transfers between devices  25.5 us (20%)
  waiting for transfers between devices  20.3 us (16%)
  Pallas kernels  13 us (10%)
  other arithmetic  6.36 us (5%)
  local copies, waits for them, and re-layouts  1.98 us (2%)
    all_to_all x1, blocking collectives, exchange(): return lax.all_to_all(value, DP, split_axis=0, concat_axis=0, tiled=True)  42.3 us
    ppermute x7, waiting for transfers between devices, all_planes(): parts.append(lax.ppermute(plane, 'dp_1', ring))  18.4 us
    psum x2, blocking collectives, plane_sums(): return lax.psum(lax.psum(partial_value, 'dp_0'), 'dp_2')  18.4 us
    all_to_all x1, starting transfers between devices, exchange(): return lax.all_to_all(value, DP, split_axis=0, concat_axis=0, tiled=True)  13.1 us
    ppermute x7, starting transfers between devices, all_planes(): parts.append(lax.ppermute(plane, 'dp_1', ring))  12.4 us
    pallas_call x1, Pallas kernels, own_block(): pl.pallas_call(functools.partial(block_kernel, len(parts), tile), out_sha...  9.06 us
    reduce_sum x2, other arithmetic, plane_sums(): jnp.sum((direction * direction).reshape(row_blocks, block_rows, col_block...  6.36 us
  transfers between devices with their start and end apart: 8, of which 4 were waited for; matrix products, arithmetic and copies ran while one was open for 0% of the time, Pallas kernels for 0%

profile of v2, /device:TPU:1, one launch (start us, length us, event | category | flops | bytes accessed | tf_op | source)
XLA Modules:
  0.0 128.4 jit_solution(12612118173643048066)
XLA Ops:
  0.0 128.2 %conditional.1 = (bf16[32,8,4096]{2,1,0:T(8,128)(2,1)}) conditional(s32[]{:T(128)} %convert_element_type.9, (s32[2,4,32]{2,1,0:T(4,128)}, bf16[32,8,4096]{2,1,0:T(8,128)(2,1)}, f32[32,8,4096]{2,1,0:T(8,128)}, bf16[1024,1024]{1,0:T(8,128)(2,1)}, bf16[1024,1024]{1,0:T(8,128)(2,1)}) %tuple.23, (bf16[32,8,4096]{2,1,0:T(8,128)(2,1)}, ...), branch_computations={%region_0.5_spmd, %region_5.10_spmd} | conditional | flops 4304404480 | bytes 44065688 | solution.py:297
  0.0 0.0 copy-start
  0.0 0.0 copy-start.3
  0.0 6.2 %fusion.4 = f32[32,4096]{1,0:T(8,128)S(1)} fusion(f32[32,8,4096]{2,1,0:T(8,128)} %get-tuple-element.30, bf16[32,8,4096]{2,1,0:T(8,128)(2,1)} %get-tuple-element.29.grad_ref), kind=kLoop, calls=%fused_computation.6 | loop fusion | flops 9306112 | bytes 6815744 | tf_op jit(solution)/shard_map/cond/branch_0_fun/reduce_sum | solution.py:253
  6.2 0.4 reduce_sum.18
  6.6 0.1 reduce_sum.19
  6.7 0.1 reshape.19
  6.8 9.5 %psum.24 = f32[1,128]{1,0:T(1,128)S(1)} all-reduce(f32[1,128]{1,0:T(1,128)S(1)} %reshape.19), channel_id=1, replica_groups=mesh['dp_0'=4,'dp_1'=8,'dp_2'=4,'mp'=2] {'dp_0'}, use_global_device_ids=true, to_apply=%region_3.0 | all-reduce | flops 128 | bytes 1024 | tf_op jit(solution)/shard_map/cond/branch_0_fun/psum | solution.py:256
  16.4 8.9 %psum.25.refs_1_ = f32[1,128]{1,0:T(1,128)S(1)} all-reduce(f32[1,128]{1,0:T(1,128)S(1)} %psum.24), channel_id=1, replica_groups=mesh['dp_0'=4,'dp_1'=8,'dp_2'=4,'mp'=2] {'dp_2'}, use_global_device_ids=true, to_apply=%region_4.4 | all-reduce | flops 128 | bytes 1024 | tf_op jit(solution)/shard_map/cond/branch_0_fun/psum | solution.py:256
  25.2 0.0 copy-done
  25.2 0.0 copy-done.3
  25.2 2.1 %gather_rows.2 = bf16[128,8,1024]{2,1,0:T(8,128)(2,1)} custom-call(s32[2,4,32]{2,1,0:T(4,128)S(1)} %copy-done.3, bf16[32,8,4096]{2,1,0:T(8,128)(2,1)S(1)} %copy-done), custom_call_target="tpu_custom_call" | custom-call | tf_op jit(solution)/shard_map/cond/branch_0_fun/gather_rows/pallas_call | solution.py:57
  27.3 13.1 %all-to-all-start = ((bf16[128,8,1024]{2,1,0:T(8,128)(2,1)}), bf16[128,8,1024]{2,1,0:T(8,128)(2,1)S(1)}, u32[]{:S(2)}, u32[]{:S(2)}) async-start(bf16[128,8,1024]{2,1,0:T(8,128)(2,1)} %gather_rows.2), calls=%async_computation | async-start | bytes 4194304 | tf_op jit(solution)/shard_map/cond/branch_0_fun/all_to_all | solution.py:244
  40.4 1.9 %collective-permute-start.6 = (f32[1,128]{1,0:T(1,128)S(1)}, f32[1,128]{1,0:T(1,128)S(1)}, u32[]{:S(2)}, u32[]{:S(2)}) collective-permute-start(f32[1,128]{1,0:T(1,128)S(1)} %psum.25.refs_1_), channel_id=1, source_target_pairs={{0,56},{8,0},{16,8},{24,16},{32,24},{40,32},{48,40},{56,48},{1,57}... | collective-permute-start | bytes 1544 | tf_op jit(solution)/shard_map/cond/branch_0_fun/ppermute | solution.py:264
  42.3 2.0 %collective-permute-start.5 = (f32[1,128]{1,0:T(1,128)S(1)}, f32[1,128]{1,0:T(1,128)S(1)}, u32[]{:S(2)}, u32[]{:S(2)}) collective-permute-start(f32[1,128]{1,0:T(1,128)S(1)} %psum.25.refs_1_), channel_id=1, source_target_pairs={{0,48},{8,56},{16,0},{24,8},{32,16},{40,24},{48,32},{56,40},{1,49}... | collective-permute-start | bytes 1544 | tf_op jit(solution)/shard_map/cond/branch_0_fun/ppermute | solution.py:264
  44.4 1.2 collective-permute-start.4
  45.5 3.3 %collective-permute-start.3 = (f32[1,128]{1,0:T(1,128)S(1)}, f32[1,128]{1,0:T(1,128)S(1)}, u32[]{:S(2)}, u32[]{:S(2)}) collective-permute-start(f32[1,128]{1,0:T(1,128)S(1)} %psum.25.refs_1_), channel_id=1, source_target_pairs={{0,32},{8,40},{16,48},{24,56},{32,0},{40,8},{48,16},{56,24},{1,33}... | collective-permute-start | bytes 1544 | tf_op jit(solution)/shard_map/cond/branch_0_fun/ppermute | solution.py:264
  48.9 0.0 collective-permute-start.2
  48.9 17.9 %collective-permute-done.6.refs_8_ = f32[1,128]{1,0:T(1,128)S(1)} collective-permute-done((f32[1,128]{1,0:T(1,128)S(1)}, f32[1,128]{1,0:T(1,128)S(1)}, u32[]{:S(2)}, u32[]{:S(2)}) %collective-permute-start.6) | collective-permute-done | bytes 544 | tf_op jit(solution)/shard_map/cond/branch_0_fun/ppermute | solution.py:264
  66.8 0.0 collective-permute-start.1
  66.8 0.0 collective-permute-done.5.refs_7_
  66.8 3.9 %collective-permute-start = (f32[1,128]{1,0:T(1,128)S(1)}, f32[1,128]{1,0:T(1,128)S(1)}, u32[]{:S(2)}, u32[]{:S(2)}) collective-permute-start(f32[1,128]{1,0:T(1,128)S(1)} %psum.25.refs_1_), channel_id=1, source_target_pairs={{0,8},{8,16},{16,24},{24,32},{32,40},{40,48},{48,56},{56,0},{1,9},... | collective-permute-start | bytes 1544 | tf_op jit(solution)/shard_map/cond/branch_0_fun/ppermute | solution.py:264
  70.8 0.1 copy.13
  70.8 0.1 reshape.18.refs_0_
  71.0 0.0 collective-permute-done.4.refs_6_
  71.0 0.0 collective-permute-done.3.refs_5_
  71.0 0.0 collective-permute-done.2.refs_4_
  71.0 0.4 collective-permute-done.1.refs_3_
  71.3 0.1 collective-permute-done.refs_2_
  71.5 1.9 %all-to-all-done = bf16[128,8,1024]{2,1,0:T(8,128)(2,1)S(1)} async-done(((bf16[128,8,1024]{2,1,0:T(8,128)(2,1)}), bf16[128,8,1024]{2,1,0:T(8,128)(2,1)S(1)}, u32[]{:S(2)}, u32[]{:S(2)}) %all-to-all-start) | async-done | bytes 2097184 | tf_op jit(solution)/shard_map/cond/branch_0_fun/all_to_all | solution.py:244
  73.4 0.0 copy-start.2
  73.4 1.3 %copy-done.2 = bf16[128,8,1024]{2,1,0:T(8,128)(2,1)} copy-done((bf16[128,8,1024]{2,1,0:T(8,128)(2,1)}, bf16[128,8,1024]{2,1,0:T(8,128)(2,1)S(1)}, u32[]{:S(2)}) %copy-start.2) | copy-done | bytes 2097176 | tf_op jit(solution)/shard_map/cond
  74.7 9.1 %own_block.2 = bf16[1024,1024]{1,0:T(8,128)(2,1)} custom-call(s32[1,128]{1,0:T(1,128)S(1)} %reshape.18.refs_0_, f32[1,128]{1,0:T(1,128)S(1)} %psum.25.refs_1_, f32[1,128]{1,0:T(1,128)S(1)} %collective-permute-done.refs_2_, f32[1,128]{1,0:T(1,128)S(1)} %collective-permute-done.1.refs_3_, f32[1,128]{1,0:T(1,128)S(1)} %collective-permute-done.2.refs_4_, ...), custom_call_target="tpu_custom_call" | custom-call | flops 4294967296 | bytes 8388608 | tf_op jit(solution)/shard_map/cond/branch_0_fun/own_block/pallas_call | solution.py:221
  83.8 42.3 %all_to_all.16.back_ref = bf16[128,8,1024]{2,1,0:T(8,128)(2,1)S(1)} all-to-all(bf16[128,8,1024]{2,1,0:T(8,128)(2,1)} %bitcast.13), channel_id=1, replica_groups=mesh['dp_0'=4,'dp_1'=8,'dp_2'=4,'mp'=2] {'dp_0','dp_1','dp_2'}, dimensions={0} | all-to-all | bytes 4194304 | tf_op jit(solution)/shard_map/cond/branch_0_fun/all_to_all | solution.py:244
  126.1 1.9 %scatter_rows.1 = bf16[32,8,4096]{2,1,0:T(8,128)(2,1)} custom-call(s32[2,4,32]{2,1,0:T(4,128)S(1)} %copy-done.3, bf16[128,8,1024]{2,1,0:T(8,128)(2,1)S(1)} %all_to_all.16.back_ref), custom_call_target="tpu_custom_call" | custom-call | tf_op jit(solution)/shard_map/cond/branch_0_fun/scatter_rows/pallas_call | solution.py:120
  (1 shorter events, 0.0 us)
Async XLA Ops:
  0.0 25.2 %copy-start = (bf16[32,8,4096]{2,1,0:T(8,128)(2,1)S(1)}, bf16[32,8,4096]{2,1,0:T(8,128)(2,1)}, u32[]{:S(2)}) copy-start(bf16[32,8,4096]{2,1,0:T(8,128)(2,1)} %get-tuple-element.29.grad_ref) | copy-start | bytes 6291460 | tf_op jit(solution)/shard_map/cond
  0.0 25.2 %copy-start.3 = (s32[2,4,32]{2,1,0:T(4,128)S(1)}, s32[2,4,32]{2,1,0:T(4,128)}, u32[]{:S(2)}) copy-start(s32[2,4,32]{2,1,0:T(4,128)} %get-tuple-element.28.table_ref) | copy-start | bytes 3076 | tf_op jit(solution)/shard_map/cond
  27.3 46.1 %all-to-all-start = ((bf16[128,8,1024]{2,1,0:T(8,128)(2,1)}), bf16[128,8,1024]{2,1,0:T(8,128)(2,1)S(1)}, u32[]{:S(2)}, u32[]{:S(2)}) async-start(bf16[128,8,1024]{2,1,0:T(8,128)(2,1)} %gather_rows.2), calls=%async_computation | async-start | bytes 4194304 | tf_op jit(solution)/shard_map/cond/branch_0_fun/all_to_all | solution.py:244
  40.4 26.4 %collective-permute-start.6 = (f32[1,128]{1,0:T(1,128)S(1)}, f32[1,128]{1,0:T(1,128)S(1)}, u32[]{:S(2)}, u32[]{:S(2)}) collective-permute-start(f32[1,128]{1,0:T(1,128)S(1)} %psum.25.refs_1_), channel_id=1, source_target_pairs={{0,56},{8,0},{16,8},{24,16},{32,24},{40,32},{48,40},{56,48},{1,57}... | collective-permute-start | bytes 1544 | tf_op jit(solution)/shard_map/cond/branch_0_fun/ppermute | solution.py:264
  42.3 24.5 %collective-permute-start.5 = (f32[1,128]{1,0:T(1,128)S(1)}, f32[1,128]{1,0:T(1,128)S(1)}, u32[]{:S(2)}, u32[]{:S(2)}) collective-permute-start(f32[1,128]{1,0:T(1,128)S(1)} %psum.25.refs_1_), channel_id=1, source_target_pairs={{0,48},{8,56},{16,0},{24,8},{32,16},{40,24},{48,32},{56,40},{1,49}... | collective-permute-start | bytes 1544 | tf_op jit(solution)/shard_map/cond/branch_0_fun/ppermute | solution.py:264
  44.4 26.6 %collective-permute-start.4 = (f32[1,128]{1,0:T(1,128)S(1)}, f32[1,128]{1,0:T(1,128)S(1)}, u32[]{:S(2)}, u32[]{:S(2)}) collective-permute-start(f32[1,128]{1,0:T(1,128)S(1)} %psum.25.refs_1_), channel_id=1, source_target_pairs={{0,40},{8,48},{16,56},{24,0},{32,8},{40,16},{48,24},{56,32},{1,41}... | collective-permute-start | bytes 1544 | tf_op jit(solution)/shard_map/cond/branch_0_fun/ppermute | solution.py:264
  45.5 25.4 %collective-permute-start.3 = (f32[1,128]{1,0:T(1,128)S(1)}, f32[1,128]{1,0:T(1,128)S(1)}, u32[]{:S(2)}, u32[]{:S(2)}) collective-permute-start(f32[1,128]{1,0:T(1,128)S(1)} %psum.25.refs_1_), channel_id=1, source_target_pairs={{0,32},{8,40},{16,48},{24,56},{32,0},{40,8},{48,16},{56,24},{1,33}... | collective-permute-start | bytes 1544 | tf_op jit(solution)/shard_map/cond/branch_0_fun/ppermute | solution.py:264
  48.9 22.1 %collective-permute-start.2 = (f32[1,128]{1,0:T(1,128)S(1)}, f32[1,128]{1,0:T(1,128)S(1)}, u32[]{:S(2)}, u32[]{:S(2)}) collective-permute-start(f32[1,128]{1,0:T(1,128)S(1)} %psum.25.refs_1_), channel_id=1, source_target_pairs={{0,24},{8,32},{16,40},{24,48},{32,56},{40,0},{48,8},{56,16},{1,25}... | collective-permute-start | bytes 1544 | tf_op jit(solution)/shard_map/cond/branch_0_fun/ppermute | solution.py:264
  66.8 4.5 %collective-permute-start.1 = (f32[1,128]{1,0:T(1,128)S(1)}, f32[1,128]{1,0:T(1,128)S(1)}, u32[]{:S(2)}, u32[]{:S(2)}) collective-permute-start(f32[1,128]{1,0:T(1,128)S(1)} %psum.25.refs_1_), channel_id=1, source_target_pairs={{0,16},{8,24},{16,32},{24,40},{32,48},{40,56},{48,0},{56,8},{1,17}... | collective-permute-start | bytes 1544 | tf_op jit(solution)/shard_map/cond/branch_0_fun/ppermute | solution.py:264
  66.8 4.7 %collective-permute-start = (f32[1,128]{1,0:T(1,128)S(1)}, f32[1,128]{1,0:T(1,128)S(1)}, u32[]{:S(2)}, u32[]{:S(2)}) collective-permute-start(f32[1,128]{1,0:T(1,128)S(1)} %psum.25.refs_1_), channel_id=1, source_target_pairs={{0,8},{8,16},{16,24},{24,32},{32,40},{40,48},{48,56},{56,0},{1,9},... | collective-permute-start | bytes 1544 | tf_op jit(solution)/shard_map/cond/branch_0_fun/ppermute | solution.py:264
  73.4 1.3 %copy-start.2 = (bf16[128,8,1024]{2,1,0:T(8,128)(2,1)}, bf16[128,8,1024]{2,1,0:T(8,128)(2,1)S(1)}, u32[]{:S(2)}) copy-start(bf16[128,8,1024]{2,1,0:T(8,128)(2,1)S(1)} %all-to-all-done) | copy-start | bytes 6291460 | tf_op jit(solution)/shard_map/cond

commit v3 on v2

--- a/solution.py
+++ b/solution.py
@@ -24,7 +24,7 @@
     return pltpu.with_memory_space_constraint(value, pltpu.HBM)
 
 
-def gather_kernel(groups, half, table_ref, grad_ref, out_ref, held_ref, in_sem, out_sem):
+def gather_kernel(groups, half, table_hbm, grad_ref, out_ref, table_ref, held_ref, table_sem, in_sem, out_sem):
     row_blocks = grad_ref.shape[0]
     block_size = out_ref.shape[-1]
     col_blocks = grad_ref.shape[2] // block_size
@@ -34,8 +34,11 @@
         rows = pl.ds(g * group, group)
         return pltpu.make_async_copy(grad_ref.at[rows], held_ref.at[rows], in_sem.at[g])
 
+    table_load = pltpu.make_async_copy(table_hbm, table_ref, table_sem)
+    table_load.start()
     for g in range(groups):
         load(g).start()
+    table_load.wait()
     for g in range(groups):
         load(g).wait()
 
@@ -53,19 +56,21 @@
 
 
 def gather_rows(table, grad, half, slots, block_size):
-    groups = 4
+    groups = 8
     return pl.pallas_call(
         functools.partial(gather_kernel, groups, half),
         out_shape=pltpu.HBM((slots, grad.shape[1], block_size), jnp.bfloat16),
-        in_specs=[SMEM, HBM],
+        in_specs=[HBM, HBM],
         out_specs=HBM,
         scratch_shapes=[
+            pltpu.SMEM(table.shape, jnp.int32),
             pltpu.VMEM(grad.shape, jnp.bfloat16),
+            pltpu.SemaphoreType.DMA,
             pltpu.SemaphoreType.DMA((groups,)),
             pltpu.SemaphoreType.DMA,
         ],
         name="gather_rows",
-    )(table, grad)
+    )(in_hbm(table), in_hbm(grad))
 
 
 def scatter_kernel(half, table_ref, back_ref, out_ref, sem):
@@ -145,27 +150,16 @@
 def block_kernel(parts, tile, *refs):
     if parts > 0:
         table_ref, part_refs, refs = refs[0], refs[1 : 1 + parts], refs[1 + parts :]
-    rows_hbm, right_hbm, left_hbm, out_hbm, rows_ref, right_ref, left_ref, mixed_ref, shaped_ref, out_ref, sem = refs
+    rows_ref, right_hbm, left_hbm, out_ref, right_ref, left_ref, mixed_ref, shaped_ref, sem = refs[:9]
     block_size = right_hbm.shape[0]
     steps = block_size // tile
 
-    def rows_load(i):
-        rows = pl.ds(i * tile, tile)
-        return pltpu.make_async_copy(rows_hbm.at[rows], rows_ref.at[rows], sem.at[i])
-
     def right_load(i):
         cols = pl.ds(i * tile, tile)
-        return pltpu.make_async_copy(right_hbm.at[:, cols], right_ref.at[:, cols], sem.at[steps + i])
-
-    def store(i):
-        rows = pl.ds(i * tile, tile)
-        return pltpu.make_async_copy(out_ref.at[rows], out_hbm.at[rows], sem.at[i])
-
-    left_load = pltpu.make_async_copy(left_hbm, left_ref, sem.at[2 * steps])
-    right_load(0).start()
+        return pltpu.make_async_copy(right_hbm.at[:, cols], right_ref.at[:, cols], sem.at[i])
+
+    left_load = pltpu.make_async_copy(left_hbm, left_ref, sem.at[steps])
     for i in range(steps):
-        rows_load(i).start()
-    for i in range(1, steps):
         right_load(i).start()
     left_load.start()
     adam_sq = None
@@ -174,8 +168,6 @@
         for part_ref in part_refs[1:]:
             totals = totals + part_ref[...]
         adam_sq = jnp.sum(jnp.where(table_ref[...] == lax.axis_index(DP), totals, 0.0))
-    for i in range(steps):
-        rows_load(i).wait()
 
     def mix(j, carry):
         cols = pl.ds(pl.multiple_of(j * tile, tile), tile)
@@ -201,43 +193,54 @@
     else:
         factor = 1.0 / jnp.sqrt(shaped_sq + NORM_EPS)
     scale = factor[0:1, 0:1]
-
-    def finish(i, carry):
-        rows = pl.ds(pl.multiple_of(i * tile, tile), tile)
-        out_ref[rows, :] = (shaped_ref[rows, :] * scale).astype(jnp.bfloat16)
-        store(i).start()
-        return carry
-
-    lax.fori_loop(0, steps, finish, 0)
-    for i in range(steps):
-        store(i).wait()
-
-
-def own_block(rows_in, right, left, table=None, parts=()):
+    band = block_size // 4
+
+    if len(refs) == 9:
+
+        def finish(i, carry):
+            rows = pl.ds(pl.multiple_of(i * band, band), band)
+            out_ref[rows, :] = (shaped_ref[rows, :] * scale).astype(jnp.bfloat16)
+            return carry
+
+        lax.fori_loop(0, 4, finish, 0)
+    else:
+        held_ref = refs[9]
+
+        def finish(i, carry):
+            rows = pl.ds(pl.multiple_of(i * band, band), band)
+            held_ref[rows, :] = (shaped_ref[rows, :] * scale).astype(jnp.bfloat16)
+            pltpu.make_async_copy(held_ref.at[rows], out_ref.at[rows], sem.at[0]).start()
+            return carry
+
+        lax.fori_loop(0, 4, finish, 0)
+        pltpu.make_async_copy(held_ref, out_ref, sem.at[0]).wait()
+
+
+def own_block(rows_in, right, left, out_in_hbm, table=None, parts=()):
     block_size = right.shape[0]
-    tile = block_size // 4
+    tile = block_size // 2
     square = pltpu.VMEM((block_size, block_size), jnp.bfloat16)
     small = () if table is None else (table, *parts)
+    shape = (block_size, block_size)
     return pl.pallas_call(
         functools.partial(block_kernel, len(parts), tile),
-        out_shape=pltpu.HBM((block_size, block_size), jnp.bfloat16),
-        in_specs=[VMEM] * len(small) + [HBM] * 3,
-        out_specs=HBM,
+        out_shape=pltpu.HBM(shape, jnp.bfloat16) if out_in_hbm else jax.ShapeDtypeStruct(shape, jnp.bfloat16),
+        in_specs=[VMEM] * (len(small) + 1) + [HBM] * 2,
+        out_specs=HBM if out_in_hbm else VMEM,
         scratch_shapes=[
             square,
             square,
             square,
-            square,
-            pltpu.VMEM((block_size, block_size), jnp.float32),
-            square,
-            pltpu.SemaphoreType.DMA((2 * (block_size // tile) + 1,)),
-        ],
-        compiler_params=pltpu.CompilerParams(vmem_limit_bytes=32 * MIB),
+            pltpu.VMEM(shape, jnp.float32),
+            pltpu.SemaphoreType.DMA((block_size // tile + 1,)),
+        ]
+        + [square] * out_in_hbm,
+        compiler_params=pltpu.CompilerParams(vmem_limit_bytes=24 * MIB),
         name="own_block",
         cost_estimate=pl.CostEstimate(
             flops=4 * block_size**3, bytes_accessed=8 * block_size**2, transcendentals=0
         ),
-    )(*small, in_hbm(rows_in), in_hbm(right), in_hbm(left))
+    )(*small, rows_in, in_hbm(right), in_hbm(left))
 
 
 def exchange(value):
@@ -271,7 +274,7 @@
     outgoing = gather_rows(table, grad, 0, slots, block_size)
     rows_in = exchange(outgoing)
     plane = plane_sums(grad, second_moment, block_size)
-    result = own_block(rows_in.reshape(block_size, block_size), right, left)
+    result = own_block(rows_in.reshape(block_size, block_size), right, left, True)
     plane, result = lax.optimization_barrier((plane, result))
     back = exchange(result.reshape(outgoing.shape))
     return scatter_rows(table, back, 0, grad, all_planes(plane))
@@ -286,7 +289,7 @@
     rows_in = exchange(outgoing)
     own_table = jnp.transpose(table[1]).reshape(1, -1)
     result = own_block(
-        rows_in.reshape(block_size, block_size), right, left, own_table, all_planes(plane)
+        rows_in.reshape(block_size, block_size), right, left, False, own_table, all_planes(plane)
     )
     back = exchange(result.reshape(outgoing.shape))
     return scatter_rows(table, back, 1, grad)

time: 129 us -> 126 us (0.977)
  blocking collectives: 60.7 us -> 62.9 us
  Pallas kernels: 13 us -> 10.9 us
  starting transfers between devices: 25.5 us -> 24.1 us
  local copies, waits for them, and re-layouts: 1.98 us -> 0.65 us
    pallas_call x1, Pallas kernels: 9.06 us -> 6.65 us  [own_block(): pl.pallas_call(functools.partial(block_kernel, len(parts), tile), out_sha...]
    all_to_all x1, blocking collectives: 42.3 us -> 44.2 us  [exchange(): return lax.all_to_all(value, DP, split_axis=0, concat_axis=0, tiled=True)]
    all_to_all x1, starting transfers between devices: 13.1 us -> 11.7 us  [exchange(): return lax.all_to_all(value, DP, split_axis=0, concat_axis=0, tiled=True)]
    cond x6 -> x2, local copies, waits for them, and re-layouts: 1.33 us -> 0.01 us
where the time goes in v3:
time: 126 us
  blocking collectives  62.9 us (50%)
  starting transfers between devices  24.1 us (19%)
  waiting for transfers between devices  20.5 us (16%)
  Pallas kernels  10.9 us (9%)
  other arithmetic  6.16 us (5%)
    all_to_all x1, blocking collectives, exchange(): return lax.all_to_all(value, DP, split_axis=0, concat_axis=0, tiled=True)  44.2 us
    psum x2, blocking collectives, plane_sums(): return lax.psum(lax.psum(partial_value, 'dp_0'), 'dp_2')  18.6 us
    ppermute x7, waiting for transfers between devices, all_planes(): parts.append(lax.ppermute(plane, 'dp_1', ring))  18.6 us
    ppermute x7, starting transfers between devices, all_planes(): parts.append(lax.ppermute(plane, 'dp_1', ring))  12.4 us
    all_to_all x1, starting transfers between devices, exchange(): return lax.all_to_all(value, DP, split_axis=0, concat_axis=0, tiled=True)  11.7 us
    pallas_call x1, Pallas kernels, own_block(): pl.pallas_call(functools.partial(block_kernel, len(parts), tile), out_sha...  6.65 us
    reduce_sum x2, other arithmetic, plane_sums(): jnp.sum((direction * direction).reshape(row_blocks, block_rows, col_block...  6.16 us
  transfers between devices with their start and end apart: 8, of which 4 were waited for; matrix products, arithmetic and copies ran while one was open for 0% of the time, Pallas kernels for 0%

profile of v3, /device:TPU:1, one launch (start us, length us, event | category | flops | bytes accessed | tf_op | source)
XLA Modules:
  0.0 126.0 jit_solution(4885169804609139510)
XLA Ops:
  0.0 125.8 %conditional.1 = (bf16[32,8,4096]{2,1,0:T(8,128)(2,1)}) conditional(s32[]{:T(128)} %convert_element_type.9, (s32[2,4,32]{2,1,0:T(4,128)}, bf16[32,8,4096]{2,1,0:T(8,128)(2,1)}, f32[32,8,4096]{2,1,0:T(8,128)}, bf16[1024,1024]{1,0:T(8,128)(2,1)}, bf16[1024,1024]{1,0:T(8,128)(2,1)}) %tuple.23, (bf16[32,8,4096]{2,1,0:T(8,128)(2,1)}, ...), branch_computations={%region_0.5_spmd, %region_5.10_spmd} | conditional | flops 4304404480 | bytes 29382528 | solution.py:300
  0.0 6.0 %fusion.4 = f32[32,4096]{1,0:T(8,128)S(1)} fusion(f32[32,8,4096]{2,1,0:T(8,128)} %get-tuple-element.30, bf16[32,8,4096]{2,1,0:T(8,128)(2,1)} %get-tuple-element.29.grad_ref), kind=kLoop, calls=%fused_computation.6 | loop fusion | flops 9306112 | bytes 6815744 | tf_op jit(solution)/shard_map/cond/branch_0_fun/reduce_sum | solution.py:256
  6.0 0.4 reduce_sum.18
  6.4 0.1 reduce_sum.19
  6.5 0.1 reshape.19
  6.6 9.5 %psum.24 = f32[1,128]{1,0:T(1,128)S(1)} all-reduce(f32[1,128]{1,0:T(1,128)S(1)} %reshape.19), channel_id=1, replica_groups=mesh['dp_0'=4,'dp_1'=8,'dp_2'=4,'mp'=2] {'dp_0'}, use_global_device_ids=true, to_apply=%region_3.0 | all-reduce | flops 128 | bytes 1024 | tf_op jit(solution)/shard_map/cond/branch_0_fun/psum | solution.py:259
  16.2 9.1 %psum.25.refs_1_ = f32[1,128]{1,0:T(1,128)S(1)} all-reduce(f32[1,128]{1,0:T(1,128)S(1)} %psum.24), channel_id=1, replica_groups=mesh['dp_0'=4,'dp_1'=8,'dp_2'=4,'mp'=2] {'dp_2'}, use_global_device_ids=true, to_apply=%region_4.4 | all-reduce | flops 128 | bytes 1024 | tf_op jit(solution)/shard_map/cond/branch_0_fun/psum | solution.py:259
  25.3 0.0 copy-start
  25.3 2.3 %gather_rows.2 = bf16[128,8,1024]{2,1,0:T(8,128)(2,1)} custom-call(s32[2,4,32]{2,1,0:T(4,128)} %get-tuple-element.28.table_hbm.table_ref, bf16[32,8,4096]{2,1,0:T(8,128)(2,1)} %get-tuple-element.29.grad_ref), custom_call_target="tpu_custom_call" | custom-call | tf_op jit(solution)/shard_map/cond/branch_0_fun/gather_rows/pallas_call | solution.py:60
  27.6 11.7 %all-to-all-start = ((bf16[128,8,1024]{2,1,0:T(8,128)(2,1)}), bf16[128,8,1024]{2,1,0:T(8,128)(2,1)S(1)}, u32[]{:S(2)}, u32[]{:S(2)}) async-start(bf16[128,8,1024]{2,1,0:T(8,128)(2,1)} %gather_rows.2), calls=%async_computation | async-start | bytes 4194304 | tf_op jit(solution)/shard_map/cond/branch_0_fun/all_to_all | solution.py:247
  39.3 1.9 %collective-permute-start.6 = (f32[1,128]{1,0:T(1,128)S(1)}, f32[1,128]{1,0:T(1,128)S(1)}, u32[]{:S(2)}, u32[]{:S(2)}) collective-permute-start(f32[1,128]{1,0:T(1,128)S(1)} %psum.25.refs_1_), channel_id=1, source_target_pairs={{0,56},{8,0},{16,8},{24,16},{32,24},{40,32},{48,40},{56,48},{1,57}... | collective-permute-start | bytes 1544 | tf_op jit(solution)/shard_map/cond/branch_0_fun/ppermute | solution.py:267
  41.2 2.0 %collective-permute-start.5 = (f32[1,128]{1,0:T(1,128)S(1)}, f32[1,128]{1,0:T(1,128)S(1)}, u32[]{:S(2)}, u32[]{:S(2)}) collective-permute-start(f32[1,128]{1,0:T(1,128)S(1)} %psum.25.refs_1_), channel_id=1, source_target_pairs={{0,48},{8,56},{16,0},{24,8},{32,16},{40,24},{48,32},{56,40},{1,49}... | collective-permute-start | bytes 1544 | tf_op jit(solution)/shard_map/cond/branch_0_fun/ppermute | solution.py:267
  43.3 1.2 collective-permute-start.4
  44.4 3.3 %collective-permute-start.3 = (f32[1,128]{1,0:T(1,128)S(1)}, f32[1,128]{1,0:T(1,128)S(1)}, u32[]{:S(2)}, u32[]{:S(2)}) collective-permute-start(f32[1,128]{1,0:T(1,128)S(1)} %psum.25.refs_1_), channel_id=1, source_target_pairs={{0,32},{8,40},{16,48},{24,56},{32,0},{40,8},{48,16},{56,24},{1,33}... | collective-permute-start | bytes 1544 | tf_op jit(solution)/shard_map/cond/branch_0_fun/ppermute | solution.py:267
  47.8 0.0 collective-permute-start.2
  47.8 18.1 %collective-permute-done.6.refs_8_ = f32[1,128]{1,0:T(1,128)S(1)} collective-permute-done((f32[1,128]{1,0:T(1,128)S(1)}, f32[1,128]{1,0:T(1,128)S(1)}, u32[]{:S(2)}, u32[]{:S(2)}) %collective-permute-start.6) | collective-permute-done | bytes 544 | tf_op jit(solution)/shard_map/cond/branch_0_fun/ppermute | solution.py:267
  65.9 0.0 collective-permute-start.1
  65.9 0.0 collective-permute-done.5.refs_7_
  65.9 3.9 %collective-permute-start = (f32[1,128]{1,0:T(1,128)S(1)}, f32[1,128]{1,0:T(1,128)S(1)}, u32[]{:S(2)}, u32[]{:S(2)}) collective-permute-start(f32[1,128]{1,0:T(1,128)S(1)} %psum.25.refs_1_), channel_id=1, source_target_pairs={{0,8},{8,16},{16,24},{24,32},{32,40},{40,48},{48,56},{56,0},{1,9},... | collective-permute-start | bytes 1544 | tf_op jit(solution)/shard_map/cond/branch_0_fun/ppermute | solution.py:267
  69.9 0.0 copy-done
  69.9 0.1 copy.13
  69.9 0.1 reshape.18.refs_0_
  70.1 0.0 collective-permute-done.4.refs_6_
  70.1 0.0 collective-permute-done.3.refs_5_
  70.1 0.0 collective-permute-done.2.refs_4_
  70.1 0.4 collective-permute-done.1.refs_3_
  70.4 0.1 collective-permute-done.refs_2_
  70.6 1.9 %all-to-all-done = bf16[128,8,1024]{2,1,0:T(8,128)(2,1)S(1)} async-done(((bf16[128,8,1024]{2,1,0:T(8,128)(2,1)}), bf16[128,8,1024]{2,1,0:T(8,128)(2,1)S(1)}, u32[]{:S(2)}, u32[]{:S(2)}) %all-to-all-start) | async-done | bytes 2097184 | tf_op jit(solution)/shard_map/cond/branch_0_fun/all_to_all | solution.py:247
  72.5 6.7 %own_block.2 = bf16[1024,1024]{1,0:T(8,128)(2,1)S(1)} custom-call(s32[1,128]{1,0:T(1,128)S(1)} %reshape.18.refs_0_, f32[1,128]{1,0:T(1,128)S(1)} %psum.25.refs_1_, f32[1,128]{1,0:T(1,128)S(1)} %collective-permute-done.refs_2_, f32[1,128]{1,0:T(1,128)S(1)} %collective-permute-done.1.refs_3_, f32[1,128]{1,0:T(1,128)S(1)} %collective-permute-done.2.refs_4_, ...), custom_call_target="tpu_custom_call" | custom-call | flops 4294967296 | bytes 8388608 | tf_op jit(solution)/shard_map/cond/branch_0_fun/own_block/pallas_call | solution.py:225
  79.1 44.2 %all_to_all.16.back_ref = bf16[128,8,1024]{2,1,0:T(8,128)(2,1)S(1)} all-to-all(bf16[128,8,1024]{2,1,0:T(8,128)(2,1)S(1)} %bitcast.13), channel_id=1, replica_groups=mesh['dp_0'=4,'dp_1'=8,'dp_2'=4,'mp'=2] {'dp_0','dp_1','dp_2'}, dimensions={0} | all-to-all | bytes 4194304 | tf_op jit(solution)/shard_map/cond/branch_0_fun/all_to_all | solution.py:247
  123.4 1.9 %scatter_rows.1 = bf16[32,8,4096]{2,1,0:T(8,128)(2,1)} custom-call(s32[2,4,32]{2,1,0:T(4,128)S(1)} %copy-done, bf16[128,8,1024]{2,1,0:T(8,128)(2,1)S(1)} %all_to_all.16.back_ref), custom_call_target="tpu_custom_call" | custom-call | tf_op jit(solution)/shard_map/cond/branch_0_fun/scatter_rows/pallas_call | solution.py:125
  (1 shorter events, 0.0 us)
Async XLA Ops:
  25.3 44.6 %copy-start = (s32[2,4,32]{2,1,0:T(4,128)S(1)}, s32[2,4,32]{2,1,0:T(4,128)}, u32[]{:S(2)}) copy-start(s32[2,4,32]{2,1,0:T(4,128)} %get-tuple-element.28.table_hbm.table_ref) | copy-start | bytes 3076 | tf_op jit(solution)/shard_map/cond
  27.6 44.9 %all-to-all-start = ((bf16[128,8,1024]{2,1,0:T(8,128)(2,1)}), bf16[128,8,1024]{2,1,0:T(8,128)(2,1)S(1)}, u32[]{:S(2)}, u32[]{:S(2)}) async-start(bf16[128,8,1024]{2,1,0:T(8,128)(2,1)} %gather_rows.2), calls=%async_computation | async-start | bytes 4194304 | tf_op jit(solution)/shard_map/cond/branch_0_fun/all_to_all | solution.py:247
  39.3 26.6 %collective-permute-start.6 = (f32[1,128]{1,0:T(1,128)S(1)}, f32[1,128]{1,0:T(1,128)S(1)}, u32[]{:S(2)}, u32[]{:S(2)}) collective-permute-start(f32[1,128]{1,0:T(1,128)S(1)} %psum.25.refs_1_), channel_id=1, source_target_pairs={{0,56},{8,0},{16,8},{24,16},{32,24},{40,32},{48,40},{56,48},{1,57}... | collective-permute-start | bytes 1544 | tf_op jit(solution)/shard_map/cond/branch_0_fun/ppermute | solution.py:267
  41.2 24.7 %collective-permute-start.5 = (f32[1,128]{1,0:T(1,128)S(1)}, f32[1,128]{1,0:T(1,128)S(1)}, u32[]{:S(2)}, u32[]{:S(2)}) collective-permute-start(f32[1,128]{1,0:T(1,128)S(1)} %psum.25.refs_1_), channel_id=1, source_target_pairs={{0,48},{8,56},{16,0},{24,8},{32,16},{40,24},{48,32},{56,40},{1,49}... | collective-permute-start | bytes 1544 | tf_op jit(solution)/shard_map/cond/branch_0_fun/ppermute | solution.py:267
  43.3 26.8 %collective-permute-start.4 = (f32[1,128]{1,0:T(1,128)S(1)}, f32[1,128]{1,0:T(1,128)S(1)}, u32[]{:S(2)}, u32[]{:S(2)}) collective-permute-start(f32[1,128]{1,0:T(1,128)S(1)} %psum.25.refs_1_), channel_id=1, source_target_pairs={{0,40},{8,48},{16,56},{24,0},{32,8},{40,16},{48,24},{56,32},{1,41}... | collective-permute-start | bytes 1544 | tf_op jit(solution)/shard_map/cond/branch_0_fun/ppermute | solution.py:267
  44.4 25.6 %collective-permute-start.3 = (f32[1,128]{1,0:T(1,128)S(1)}, f32[1,128]{1,0:T(1,128)S(1)}, u32[]{:S(2)}, u32[]{:S(2)}) collective-permute-start(f32[1,128]{1,0:T(1,128)S(1)} %psum.25.refs_1_), channel_id=1, source_target_pairs={{0,32},{8,40},{16,48},{24,56},{32,0},{40,8},{48,16},{56,24},{1,33}... | collective-permute-start | bytes 1544 | tf_op jit(solution)/shard_map/cond/branch_0_fun/ppermute | solution.py:267
  47.8 22.3 %collective-permute-start.2 = (f32[1,128]{1,0:T(1,128)S(1)}, f32[1,128]{1,0:T(1,128)S(1)}, u32[]{:S(2)}, u32[]{:S(2)}) collective-permute-start(f32[1,128]{1,0:T(1,128)S(1)} %psum.25.refs_1_), channel_id=1, source_target_pairs={{0,24},{8,32},{16,40},{24,48},{32,56},{40,0},{48,8},{56,16},{1,25}... | collective-permute-start | bytes 1544 | tf_op jit(solution)/shard_map/cond/branch_0_fun/ppermute | solution.py:267
  65.9 4.5 %collective-permute-start.1 = (f32[1,128]{1,0:T(1,128)S(1)}, f32[1,128]{1,0:T(1,128)S(1)}, u32[]{:S(2)}, u32[]{:S(2)}) collective-permute-start(f32[1,128]{1,0:T(1,128)S(1)} %psum.25.refs_1_), channel_id=1, source_target_pairs={{0,16},{8,24},{16,32},{24,40},{32,48},{40,56},{48,0},{56,8},{1,17}... | collective-permute-start | bytes 1544 | tf_op jit(solution)/shard_map/cond/branch_0_fun/ppermute | solution.py:267
  65.9 4.7 %collective-permute-start = (f32[1,128]{1,0:T(1,128)S(1)}, f32[1,128]{1,0:T(1,128)S(1)}, u32[]{:S(2)}, u32[]{:S(2)}) collective-permute-start(f32[1,128]{1,0:T(1,128)S(1)} %psum.25.refs_1_), channel_id=1, source_target_pairs={{0,8},{8,16},{16,24},{24,32},{32,40},{40,48},{48,56},{56,0},{1,9},... | collective-permute-start | bytes 1544 | tf_op jit(solution)/shard_map/cond/branch_0_fun/ppermute | solution.py:267

commit v4 on v3

--- a/solution.py
+++ b/solution.py
@@ -147,10 +147,29 @@
     )(table, *parts, back)
 
 
+def fetch_kernel(after_ref, right_hbm, out_ref, sem):
+    columns = right_hbm.at[:, pl.ds(0, out_ref.shape[1])]
+    copy = pltpu.make_async_copy(columns, out_ref, sem)
+    copy.start()
+    copy.wait()
+
+
+def fetch_columns(after, right, columns):
+    return pl.pallas_call(
+        fetch_kernel,
+        out_shape=jax.ShapeDtypeStruct((right.shape[0], columns), jnp.bfloat16),
+        in_specs=[VMEM, HBM],
+        out_specs=VMEM,
+        scratch_shapes=[pltpu.SemaphoreType.DMA],
+        compiler_params=pltpu.CompilerParams(vmem_limit_bytes=8 * MIB),
+        name="fetch_columns",
+    )(after, in_hbm(right))
+
+
 def block_kernel(parts, tile, *refs):
     if parts > 0:
         table_ref, part_refs, refs = refs[0], refs[1 : 1 + parts], refs[1 + parts :]
-    rows_ref, right_hbm, left_hbm, out_ref, right_ref, left_ref, mixed_ref, shaped_ref, sem = refs[:9]
+    rows_ref, first_ref, right_hbm, left_hbm, out_ref, right_ref, left_ref, mixed_ref, shaped_ref, sem = refs[:10]
     block_size = right_hbm.shape[0]
     steps = block_size // tile
 
@@ -159,7 +178,7 @@
         return pltpu.make_async_copy(right_hbm.at[:, cols], right_ref.at[:, cols], sem.at[i])
 
     left_load = pltpu.make_async_copy(left_hbm, left_ref, sem.at[steps])
-    for i in range(steps):
+    for i in range(1, steps):
         right_load(i).start()
     left_load.start()
     adam_sq = None
@@ -169,15 +188,14 @@
             totals = totals + part_ref[...]
         adam_sq = jnp.sum(jnp.where(table_ref[...] == lax.axis_index(DP), totals, 0.0))
 
-    def mix(j, carry):
-        cols = pl.ds(pl.multiple_of(j * tile, tile), tile)
-        right_load(j).wait()
+    for j in range(steps):
+        cols = pl.ds(j * tile, tile)
+        if j > 0:
+            right_load(j).wait()
+        columns = right_ref[:, cols] if j > 0 else first_ref[...]
         mixed_ref[:, cols] = jnp.dot(
-            rows_ref[...], right_ref[:, cols], preferred_element_type=jnp.float32
+            rows_ref[...], columns, preferred_element_type=jnp.float32
         ).astype(jnp.bfloat16)
-        return carry
-
-    lax.fori_loop(0, steps, mix, 0)
     left_load.wait()
 
     def shape(j, squares):
@@ -195,7 +213,7 @@
     scale = factor[0:1, 0:1]
     band = block_size // 4
 
-    if len(refs) == 9:
+    if len(refs) == 10:
 
         def finish(i, carry):
             rows = pl.ds(pl.multiple_of(i * band, band), band)
@@ -204,7 +222,7 @@
 
         lax.fori_loop(0, 4, finish, 0)
     else:
-        held_ref = refs[9]
+        held_ref = refs[10]
 
         def finish(i, carry):
             rows = pl.ds(pl.multiple_of(i * band, band), band)
@@ -216,16 +234,16 @@
         pltpu.make_async_copy(held_ref, out_ref, sem.at[0]).wait()
 
 
-def own_block(rows_in, right, left, out_in_hbm, table=None, parts=()):
+def own_block(rows_in, first, right, left, out_in_hbm, table=None, parts=()):
     block_size = right.shape[0]
-    tile = block_size // 2
+    tile = first.shape[1]
     square = pltpu.VMEM((block_size, block_size), jnp.bfloat16)
     small = () if table is None else (table, *parts)
     shape = (block_size, block_size)
     return pl.pallas_call(
         functools.partial(block_kernel, len(parts), tile),
         out_shape=pltpu.HBM(shape, jnp.bfloat16) if out_in_hbm else jax.ShapeDtypeStruct(shape, jnp.bfloat16),
-        in_specs=[VMEM] * (len(small) + 1) + [HBM] * 2,
+        in_specs=[VMEM] * (len(small) + 2) + [HBM] * 2,
         out_specs=HBM if out_in_hbm else VMEM,
         scratch_shapes=[
             square,
@@ -240,7 +258,7 @@
         cost_estimate=pl.CostEstimate(
             flops=4 * block_size**3, bytes_accessed=8 * block_size**2, transcendentals=0
         ),
-    )(*small, rows_in, in_hbm(right), in_hbm(left))
+    )(*small, rows_in, first, in_hbm(right), in_hbm(left))
 
 
 def exchange(value):
@@ -274,7 +292,8 @@
     outgoing = gather_rows(table, grad, 0, slots, block_size)
     rows_in = exchange(outgoing)
     plane = plane_sums(grad, second_moment, block_size)
-    result = own_block(rows_in.reshape(block_size, block_size), right, left, True)
+    first = fetch_columns(plane, right, block_size // 2)
+    result = own_block(rows_in.reshape(block_size, block_size), first, right, left, True)
     plane, result = lax.optimization_barrier((plane, result))
     back = exchange(result.reshape(outgoing.shape))
     return scatter_rows(table, back, 0, grad, all_planes(plane))
@@ -285,11 +304,13 @@
     slots = lax.axis_size(DP)
     outgoing = gather_rows(table, grad, 1, slots, block_size)
     plane = plane_sums(grad, second_moment, block_size)
-    plane, outgoing = lax.optimization_barrier((plane, outgoing))
+    parts = all_planes(plane)
+    *parts[:3], outgoing = lax.optimization_barrier((*parts[:3], outgoing))
     rows_in = exchange(outgoing)
     own_table = jnp.transpose(table[1]).reshape(1, -1)
+    first = fetch_columns(parts[-1], right, block_size // 2)
     result = own_block(
-        rows_in.reshape(block_size, block_size), right, left, False, own_table, all_planes(plane)
+        rows_in.reshape(block_size, block_size), first, right, left, False, own_table, parts
     )
     back = exchange(result.reshape(outgoing.shape))
     return scatter_rows(table, back, 1, grad)

time: 126 us -> 122 us (0.968)
  blocking collectives: 62.9 us -> 57.6 us
    all_to_all x1, blocking collectives: 44.2 us -> 39 us  [exchange(): return lax.all_to_all(value, DP, split_axis=0, concat_axis=0, tiled=True)]
    all_to_all x1, starting transfers between devices: 11.7 us -> 9 us  [exchange(): return lax.all_to_all(value, DP, split_axis=0, concat_axis=0, tiled=True)]
    ppermute x7, starting transfers between devices: 12.4 us -> 14.7 us  [all_planes(): parts.append(lax.ppermute(plane, 'dp_1', ring))]
    all_to_all x1, waiting for transfers between devices: 1.91 us -> 3.99 us  [exchange(): return lax.all_to_all(value, DP, split_axis=0, concat_axis=0, tiled=True)]
    ppermute x7, waiting for transfers between devices: 18.6 us -> 17.1 us  [all_planes(): parts.append(lax.ppermute(plane, 'dp_1', ring))]
  transfers between devices with their start and end apart: 8 -> 8, of which waited for: 4 -> 5; matrix products, arithmetic and copies ran while one was open for 0% -> 0% of each run, Pallas kernels for 0% -> 3%
where the time goes in v4:
time: 122 us
  blocking collectives  57.6 us (47%)
  starting transfers between devices  23.7 us (19%)
  waiting for transfers between devices  21.1 us (17%)
  Pallas kernels  11.9 us (10%)
  other arithmetic  6.16 us (5%)
    all_to_all x1, blocking collectives, exchange(): return lax.all_to_all(value, DP, split_axis=0, concat_axis=0, tiled=True)  39 us
    psum x2, blocking collectives, plane_sums(): return lax.psum(lax.psum(partial_value, 'dp_0'), 'dp_2')  18.6 us
    ppermute x7, waiting for transfers between devices, all_planes(): parts.append(lax.ppermute(plane, 'dp_1', ring))  17.1 us
    ppermute x7, starting transfers between devices, all_planes(): parts.append(lax.ppermute(plane, 'dp_1', ring))  14.7 us
    all_to_all x1, starting transfers between devices, exchange(): return lax.all_to_all(value, DP, split_axis=0, concat_axis=0, tiled=True)  9 us
    pallas_call x1, Pallas kernels, own_block(): pl.pallas_call(functools.partial(block_kernel, len(parts), tile), out_sha...  6.45 us
    reduce_sum x2, other arithmetic, plane_sums(): jnp.sum((direction * direction).reshape(row_blocks, block_rows, col_block...  6.16 us
    all_to_all x1, waiting for transfers between devices, exchange(): return lax.all_to_all(value, DP, split_axis=0, concat_axis=0, tiled=True)  3.99 us
  transfers between devices with their start and end apart: 8, of which 5 were waited for; matrix products, arithmetic and copies ran while one was open for 0% of the time, Pallas kernels for 3%

profile of v4, /device:TPU:1, one launch (start us, length us, event | category | flops | bytes accessed | tf_op | source)
XLA Modules:
  0.0 121.9 jit_solution(16699774439796911253)
XLA Ops:
  0.0 121.7 %conditional.1 = (bf16[32,8,4096]{2,1,0:T(8,128)(2,1)}) conditional(s32[]{:T(128)} %convert_element_type.9, (s32[2,4,32]{2,1,0:T(4,128)}, bf16[32,8,4096]{2,1,0:T(8,128)(2,1)}, f32[32,8,4096]{2,1,0:T(8,128)}, bf16[1024,1024]{1,0:T(8,128)(2,1)}, bf16[1024,1024]{1,0:T(8,128)(2,1)}) %tuple.23, (bf16[32,8,4096]{2,1,0:T(8,128)(2,1)}, ...), branch_computations={%region_0.5_spmd, %region_5.10_spmd} | conditional | flops 4304404480 | bytes 29382528 | solution.py:321
  0.0 6.0 %fusion.4 = f32[32,4096]{1,0:T(8,128)S(1)} fusion(f32[32,8,4096]{2,1,0:T(8,128)} %get-tuple-element.30, bf16[32,8,4096]{2,1,0:T(8,128)(2,1)} %get-tuple-element.29.grad_ref), kind=kLoop, calls=%fused_computation.6 | loop fusion | flops 9306112 | bytes 6815744 | tf_op jit(solution)/shard_map/cond/branch_0_fun/reduce_sum | solution.py:274
  6.0 0.4 reduce_sum.18
  6.4 0.1 reduce_sum.19
  6.5 0.1 reshape.19
  6.6 9.5 %psum.24 = f32[1,128]{1,0:T(1,128)S(1)} all-reduce(f32[1,128]{1,0:T(1,128)S(1)} %reshape.19), channel_id=1, replica_groups=mesh['dp_0'=4,'dp_1'=8,'dp_2'=4,'mp'=2] {'dp_0'}, use_global_device_ids=true, to_apply=%region_3.0 | all-reduce | flops 128 | bytes 1024 | tf_op jit(solution)/shard_map/cond/branch_0_fun/psum | solution.py:277
  16.2 9.1 %psum.25.refs_1_ = f32[1,128]{1,0:T(1,128)S(1)} all-reduce(f32[1,128]{1,0:T(1,128)S(1)} %psum.24), channel_id=1, replica_groups=mesh['dp_0'=4,'dp_1'=8,'dp_2'=4,'mp'=2] {'dp_2'}, use_global_device_ids=true, to_apply=%region_4.4 | all-reduce | flops 128 | bytes 1024 | tf_op jit(solution)/shard_map/cond/branch_0_fun/psum | solution.py:277
  25.3 1.7 %collective-permute-start = (f32[1,128]{1,0:T(1,128)S(1)}, f32[1,128]{1,0:T(1,128)S(1)}, u32[]{:S(2)}, u32[]{:S(2)}) collective-permute-start(f32[1,128]{1,0:T(1,128)S(1)} %psum.25.refs_1_), channel_id=1, source_target_pairs={{0,8},{8,16},{16,24},{24,32},{32,40},{40,48},{48,56},{56,0},{1,9},... | collective-permute-start | bytes 1544 | tf_op jit(solution)/shard_map/cond/branch_0_fun/ppermute | solution.py:285
  27.0 3.4 %collective-permute-start.1 = (f32[1,128]{1,0:T(1,128)S(1)}, f32[1,128]{1,0:T(1,128)S(1)}, u32[]{:S(2)}, u32[]{:S(2)}) collective-permute-start(f32[1,128]{1,0:T(1,128)S(1)} %psum.25.refs_1_), channel_id=1, source_target_pairs={{0,16},{8,24},{16,32},{24,40},{32,48},{40,56},{48,0},{56,8},{1,17}... | collective-permute-start | bytes 1544 | tf_op jit(solution)/shard_map/cond/branch_0_fun/ppermute | solution.py:285
  30.4 0.0 copy-start
  30.4 2.3 %gather_rows.2 = bf16[128,8,1024]{2,1,0:T(8,128)(2,1)} custom-call(s32[2,4,32]{2,1,0:T(4,128)} %get-tuple-element.28.table_hbm.table_ref, bf16[32,8,4096]{2,1,0:T(8,128)(2,1)} %get-tuple-element.29.grad_ref), custom_call_target="tpu_custom_call" | custom-call | tf_op jit(solution)/shard_map/cond/branch_0_fun/gather_rows/pallas_call | solution.py:60
  32.7 0.0 collective-permute-done.refs_2_
  32.7 0.7 collective-permute-done.1.refs_3_
  33.4 9.0 %all-to-all-start = ((bf16[128,8,1024]{2,1,0:T(8,128)(2,1)}), bf16[128,8,1024]{2,1,0:T(8,128)(2,1)S(1)}, u32[]{:S(2)}, u32[]{:S(2)}) async-start(bf16[128,8,1024]{2,1,0:T(8,128)(2,1)} %gather_rows.2), calls=%async_computation | async-start | bytes 4194304 | tf_op jit(solution)/shard_map/cond/branch_0_fun/all_to_all | solution.py:265
  42.4 2.5 %collective-permute-start.2 = (f32[1,128]{1,0:T(1,128)S(1)}, f32[1,128]{1,0:T(1,128)S(1)}, u32[]{:S(2)}, u32[]{:S(2)}) collective-permute-start(f32[1,128]{1,0:T(1,128)S(1)} %psum.25.refs_1_), channel_id=1, source_target_pairs={{0,24},{8,32},{16,40},{24,48},{32,56},{40,0},{48,8},{56,16},{1,25}... | collective-permute-start | bytes 1544 | tf_op jit(solution)/shard_map/cond/branch_0_fun/ppermute | solution.py:285
  44.9 2.5 %collective-permute-start.3 = (f32[1,128]{1,0:T(1,128)S(1)}, f32[1,128]{1,0:T(1,128)S(1)}, u32[]{:S(2)}, u32[]{:S(2)}) collective-permute-start(f32[1,128]{1,0:T(1,128)S(1)} %psum.25.refs_1_), channel_id=1, source_target_pairs={{0,32},{8,40},{16,48},{24,56},{32,0},{40,8},{48,16},{56,24},{1,33}... | collective-permute-start | bytes 1544 | tf_op jit(solution)/shard_map/cond/branch_0_fun/ppermute | solution.py:285
  47.3 4.1 %collective-permute-start.4 = (f32[1,128]{1,0:T(1,128)S(1)}, f32[1,128]{1,0:T(1,128)S(1)}, u32[]{:S(2)}, u32[]{:S(2)}) collective-permute-start(f32[1,128]{1,0:T(1,128)S(1)} %psum.25.refs_1_), channel_id=1, source_target_pairs={{0,40},{8,48},{16,56},{24,0},{32,8},{40,16},{48,24},{56,32},{1,41}... | collective-permute-start | bytes 1544 | tf_op jit(solution)/shard_map/cond/branch_0_fun/ppermute | solution.py:285
  51.5 0.3 collective-permute-start.5
  51.7 0.3 collective-permute-start.6
  52.0 0.0 copy-done
  52.0 0.1 copy.13
  52.1 0.1 reshape.18.refs_0_
  52.2 12.4 %collective-permute-done.6.after_ref.refs_8_ = f32[1,128]{1,0:T(1,128)S(1)} collective-permute-done((f32[1,128]{1,0:T(1,128)S(1)}, f32[1,128]{1,0:T(1,128)S(1)}, u32[]{:S(2)}, u32[]{:S(2)}) %collective-permute-start.6) | collective-permute-done | bytes 544 | tf_op jit(solution)/shard_map/cond/branch_0_fun/ppermute | solution.py:285
  64.7 1.2 %fetch_columns.2.refs_10_ = bf16[1024,512]{1,0:T(8,128)(2,1)S(1)} custom-call(f32[1,128]{1,0:T(1,128)S(1)} %collective-permute-done.6.after_ref.refs_8_, bf16[1024,1024]{1,0:T(8,128)(2,1)} %get-tuple-element.35.right_hbm.refs_11_), custom_call_target="tpu_custom_call" | custom-call | tf_op jit(solution)/shard_map/cond/branch_0_fun/fetch_columns/pallas_call | solution.py:158
  65.9 2.9 %collective-permute-done.2.refs_4_ = f32[1,128]{1,0:T(1,128)S(1)} collective-permute-done((f32[1,128]{1,0:T(1,128)S(1)}, f32[1,128]{1,0:T(1,128)S(1)}, u32[]{:S(2)}, u32[]{:S(2)}) %collective-permute-start.2) | collective-permute-done | bytes 544 | tf_op jit(solution)/shard_map/cond/branch_0_fun/ppermute | solution.py:285
  68.8 1.0 collective-permute-done.3.refs_5_
  69.8 0.0 collective-permute-done.4.refs_6_
  69.8 0.0 collective-permute-done.5.refs_7_
  69.8 4.0 %all-to-all-done = bf16[128,8,1024]{2,1,0:T(8,128)(2,1)S(1)} async-done(((bf16[128,8,1024]{2,1,0:T(8,128)(2,1)}), bf16[128,8,1024]{2,1,0:T(8,128)(2,1)S(1)}, u32[]{:S(2)}, u32[]{:S(2)}) %all-to-all-start) | async-done | bytes 2097184 | tf_op jit(solution)/shard_map/cond/branch_0_fun/all_to_all | solution.py:265
  73.8 6.4 %own_block.2 = bf16[1024,1024]{1,0:T(8,128)(2,1)S(1)} custom-call(s32[1,128]{1,0:T(1,128)S(1)} %reshape.18.refs_0_, f32[1,128]{1,0:T(1,128)S(1)} %psum.25.refs_1_, f32[1,128]{1,0:T(1,128)S(1)} %collective-permute-done.refs_2_, f32[1,128]{1,0:T(1,128)S(1)} %collective-permute-done.1.refs_3_, f32[1,128]{1,0:T(1,128)S(1)} %collective-permute-done.2.refs_4_, ...), custom_call_target="tpu_custom_call" | custom-call | flops 4294967296 | bytes 8388608 | tf_op jit(solution)/shard_map/cond/branch_0_fun/own_block/pallas_call | solution.py:243
  80.3 39.0 %all_to_all.16.back_ref = bf16[128,8,1024]{2,1,0:T(8,128)(2,1)S(1)} all-to-all(bf16[128,8,1024]{2,1,0:T(8,128)(2,1)S(1)} %bitcast.13), channel_id=1, replica_groups=mesh['dp_0'=4,'dp_1'=8,'dp_2'=4,'mp'=2] {'dp_0','dp_1','dp_2'}, dimensions={0} | all-to-all | bytes 4194304 | tf_op jit(solution)/shard_map/cond/branch_0_fun/all_to_all | solution.py:265
  119.3 1.9 %scatter_rows.1 = bf16[32,8,4096]{2,1,0:T(8,128)(2,1)} custom-call(s32[2,4,32]{2,1,0:T(4,128)S(1)} %copy-done, bf16[128,8,1024]{2,1,0:T(8,128)(2,1)S(1)} %all_to_all.16.back_ref), custom_call_target="tpu_custom_call" | custom-call | tf_op jit(solution)/shard_map/cond/branch_0_fun/scatter_rows/pallas_call | solution.py:125
  (1 shorter events, 0.0 us)
Async XLA Ops:
  25.3 7.4 %collective-permute-start = (f32[1,128]{1,0:T(1,128)S(1)}, f32[1,128]{1,0:T(1,128)S(1)}, u32[]{:S(2)}, u32[]{:S(2)}) collective-permute-start(f32[1,128]{1,0:T(1,128)S(1)} %psum.25.refs_1_), channel_id=1, source_target_pairs={{0,8},{8,16},{16,24},{24,32},{32,40},{40,48},{48,56},{56,0},{1,9},... | collective-permute-start | bytes 1544 | tf_op jit(solution)/shard_map/cond/branch_0_fun/ppermute | solution.py:285
  27.0 6.4 %collective-permute-start.1 = (f32[1,128]{1,0:T(1,128)S(1)}, f32[1,128]{1,0:T(1,128)S(1)}, u32[]{:S(2)}, u32[]{:S(2)}) collective-permute-start(f32[1,128]{1,0:T(1,128)S(1)} %psum.25.refs_1_), channel_id=1, source_target_pairs={{0,16},{8,24},{16,32},{24,40},{32,48},{40,56},{48,0},{56,8},{1,17}... | collective-permute-start | bytes 1544 | tf_op jit(solution)/shard_map/cond/branch_0_fun/ppermute | solution.py:285
  30.4 21.7 %copy-start = (s32[2,4,32]{2,1,0:T(4,128)S(1)}, s32[2,4,32]{2,1,0:T(4,128)}, u32[]{:S(2)}) copy-start(s32[2,4,32]{2,1,0:T(4,128)} %get-tuple-element.28.table_hbm.table_ref) | copy-start | bytes 3076 | tf_op jit(solution)/shard_map/cond
  33.4 40.4 %all-to-all-start = ((bf16[128,8,1024]{2,1,0:T(8,128)(2,1)}), bf16[128,8,1024]{2,1,0:T(8,128)(2,1)S(1)}, u32[]{:S(2)}, u32[]{:S(2)}) async-start(bf16[128,8,1024]{2,1,0:T(8,128)(2,1)} %gather_rows.2), calls=%async_computation | async-start | bytes 4194304 | tf_op jit(solution)/shard_map/cond/branch_0_fun/all_to_all | solution.py:265
  42.4 26.4 %collective-permute-start.2 = (f32[1,128]{1,0:T(1,128)S(1)}, f32[1,128]{1,0:T(1,128)S(1)}, u32[]{:S(2)}, u32[]{:S(2)}) collective-permute-start(f32[1,128]{1,0:T(1,128)S(1)} %psum.25.refs_1_), channel_id=1, source_target_pairs={{0,24},{8,32},{16,40},{24,48},{32,56},{40,0},{48,8},{56,16},{1,25}... | collective-permute-start | bytes 1544 | tf_op jit(solution)/shard_map/cond/branch_0_fun/ppermute | solution.py:285
  44.9 25.0 %collective-permute-start.3 = (f32[1,128]{1,0:T(1,128)S(1)}, f32[1,128]{1,0:T(1,128)S(1)}, u32[]{:S(2)}, u32[]{:S(2)}) collective-permute-start(f32[1,128]{1,0:T(1,128)S(1)} %psum.25.refs_1_), channel_id=1, source_target_pairs={{0,32},{8,40},{16,48},{24,56},{32,0},{40,8},{48,16},{56,24},{1,33}... | collective-permute-start | bytes 1544 | tf_op jit(solution)/shard_map/cond/branch_0_fun/ppermute | solution.py:285
  47.3 22.5 %collective-permute-start.4 = (f32[1,128]{1,0:T(1,128)S(1)}, f32[1,128]{1,0:T(1,128)S(1)}, u32[]{:S(2)}, u32[]{:S(2)}) collective-permute-start(f32[1,128]{1,0:T(1,128)S(1)} %psum.25.refs_1_), channel_id=1, source_target_pairs={{0,40},{8,48},{16,56},{24,0},{32,8},{40,16},{48,24},{56,32},{1,41}... | collective-permute-start | bytes 1544 | tf_op jit(solution)/shard_map/cond/branch_0_fun/ppermute | solution.py:285
  51.5 18.4 %collective-permute-start.5 = (f32[1,128]{1,0:T(1,128)S(1)}, f32[1,128]{1,0:T(1,128)S(1)}, u32[]{:S(2)}, u32[]{:S(2)}) collective-permute-start(f32[1,128]{1,0:T(1,128)S(1)} %psum.25.refs_1_), channel_id=1, source_target_pairs={{0,48},{8,56},{16,0},{24,8},{32,16},{40,24},{48,32},{56,40},{1,49}... | collective-permute-start | bytes 1544 | tf_op jit(solution)/shard_map/cond/branch_0_fun/ppermute | solution.py:285
  51.7 12.9 %collective-permute-start.6 = (f32[1,128]{1,0:T(1,128)S(1)}, f32[1,128]{1,0:T(1,128)S(1)}, u32[]{:S(2)}, u32[]{:S(2)}) collective-permute-start(f32[1,128]{1,0:T(1,128)S(1)} %psum.25.refs_1_), channel_id=1, source_target_pairs={{0,56},{8,0},{16,8},{24,16},{32,24},{40,32},{48,40},{56,48},{1,57}... | collective-permute-start | bytes 1544 | tf_op jit(solution)/shard_map/cond/branch_0_fun/ppermute | solution.py:285

commit v5 on v4

v5 whole, which is shorter than its diff:
```python
import functools

import jax
import jax.numpy as jnp
from jax import lax
from jax.experimental import pallas as pl
from jax.experimental.pallas import tpu as pltpu
from jax.sharding import Mesh
from jax.sharding import PartitionSpec as P

DP = ("dp_0", "dp_1", "dp_2")


BETA_TWO = 0.99
ADAM_EPS = 1e-08
NORM_EPS = 1e-06
MIB = 1 << 20
VMEM = pl.BlockSpec(memory_space=pltpu.VMEM)
HBM = pl.BlockSpec(memory_space=pltpu.HBM)
SMEM = pl.BlockSpec(memory_space=pltpu.SMEM)


def in_hbm(value):
    return pltpu.with_memory_space_constraint(value, pltpu.HBM)


def gather_kernel(groups, half, table_hbm, grad_hbm, *refs):
    in_vmem = len(refs) > 6
    if in_vmem:
        right_hbm, out_ref, first_ref, table_ref, held_ref, table_sem, in_sem, out_sem = refs
    else:
        out_ref, table_ref, held_ref, table_sem, in_sem, out_sem = refs
    row_blocks = grad_hbm.shape[0]
    block_size = out_ref.shape[-1]
    col_blocks = grad_hbm.shape[2] // block_size
    group = row_blocks // groups

    def load(g):
        rows = pl.ds(g * group, group)
        return pltpu.make_async_copy(grad_hbm.at[rows], held_ref.at[rows], in_sem.at[g])

    table_load = pltpu.make_async_copy(table_hbm, table_ref, table_sem)
    table_load.start()
    for g in range(groups):
        load(g).start()
    if in_vmem:
        columns = right_hbm.at[:, pl.ds(0, first_ref.shape[1])]
        first_load = pltpu.make_async_copy(columns, first_ref, out_sem)
        first_load.start()
    table_load.wait()
    for g in range(groups):
        load(g).wait()

        def one_row(row, carry):
            for col in range(col_blocks):
                columns = pl.ds(col * block_size, block_size)
                slot = table_ref[half, col, row]
                if in_vmem:
                    out_ref[slot] = held_ref[row, :, columns]
                else:
                    pltpu.make_async_copy(held_ref.at[row, :, columns], out_ref.at[slot], out_sem).start()
            return carry

        lax.fori_loop(g * group, (g + 1) * group, one_row, 0)
    if in_vmem:
        first_load.wait()
    else:
        pltpu.make_async_copy(out_ref, out_ref, out_sem).wait()


def gather_rows(table, grad, half, slots, block_size, right=None):
    groups = 8
    shape = (slots, grad.shape[1], block_size)
    in_vmem = right is not None
    if in_vmem:
        rows = jax.ShapeDtypeStruct(shape, jnp.bfloat16)
        out_shape = (rows, jax.ShapeDtypeStruct((block_size, block_size // 2), jnp.bfloat16))
    else:
        out_shape = pltpu.HBM(shape, jnp.bfloat16)
    return pl.pallas_call(
        functools.partial(gather_kernel, groups, half),
        out_shape=out_shape,
        in_specs=[HBM, HBM] + [HBM] * in_vmem,
        out_specs=(VMEM, VMEM) if in_vmem else HBM,
        scratch_shapes=[
            pltpu.SMEM(table.shape, jnp.int32),
            pltpu.VMEM(grad.shape, jnp.bfloat16),
            pltpu.SemaphoreType.DMA,
            pltpu.SemaphoreType.DMA((groups,)),
            pltpu.SemaphoreType.DMA,
        ],
        compiler_params=pltpu.CompilerParams(vmem_limit_bytes=12 * MIB),
        name="gather_rows",
    )(in_hbm(table), in_hbm(grad), *([in_hbm(right)] if in_vmem else []))


def scatter_kernel(half, table_ref, back_ref, out_ref, held_ref, sem):
    row_blocks = out_ref.shape[0]
    block_size = back_ref.shape[-1]
    col_blocks = out_ref.shape[2] // block_size

    def one_row(row, carry):
        for col in range(col_blocks):
            columns = pl.ds(col * block_size, block_size)
            held_ref[row, :, columns] = back_ref[table_ref[half, col, row]]
        pltpu.make_async_copy(held_ref.at[row], out_ref.at[row], sem).start()
        return carry

    lax.fori_loop(0, row_blocks, one_row, 0)
    pltpu.make_async_copy(out_ref, out_ref, sem).wait()


def scaled_scatter_kernel(parts, half, table_ref, *refs):
    part_refs = refs[:parts]
    back_ref, out_ref, norm_ref, held_ref, sem = refs[parts:]
    row_blocks = out_ref.shape[0]
    block_size = back_ref.shape[-1]
    col_blocks = out_ref.shape[2] // block_size
    blocks = row_blocks * col_blocks
    totals = part_refs[0][...]
    for part_ref in part_refs[1:]:
        totals = totals + part_ref[...]
    norms = jnp.sqrt((totals[0:1] + NORM_EPS) / (totals[1:2] + NORM_EPS))
    norm_ref[...] = jnp.transpose(jnp.broadcast_to(norms, (blocks, blocks)))

    def one_row(row, carry):
        for col in range(col_blocks):
            slot = table_ref[half, col, row]
            norm = norm_ref[pl.ds(col * row_blocks + row, 1), :]
            norm = jnp.concatenate([norm] * (block_size // blocks), axis=1)
            rows = back_ref[slot].astype(jnp.float32) * norm
            held_ref[row, :, pl.ds(col * block_size, block_size)] = rows.astype(jnp.bfloat16)
        pltpu.make_async_copy(held_ref.at[row], out_ref.at[row], sem).start()
        return carry

    lax.fori_loop(0, row_blocks, one_row, 0)
    pltpu.make_async_copy(out_ref, out_ref, sem).wait()


def scatter_rows(table, back, half, like, parts=None):
    out_shape = pltpu.HBM(like.shape, jnp.bfloat16)
    params = pltpu.CompilerParams(vmem_limit_bytes=8 * MIB)
    if parts is None:
        return pl.pallas_call(
            functools.partial(scatter_kernel, half),
            out_shape=out_shape,
            in_specs=[SMEM, VMEM],
            out_specs=HBM,
            scratch_shapes=[pltpu.VMEM(like.shape, jnp.bfloat16), pltpu.SemaphoreType.DMA],
            compiler_params=params,
            name="scatter_rows",
        )(table, back)
    blocks = parts[0].shape[1]
    return pl.pallas_call(
        functools.partial(scaled_scatter_kernel, len(parts), half),
        out_shape=out_shape,
        in_specs=[SMEM] + [VMEM] * (len(parts) + 1),
        out_specs=HBM,
        scratch_shapes=[
            pltpu.VMEM((blocks, blocks), jnp.float32),
            pltpu.VMEM(like.shape, jnp.bfloat16),
            pltpu.SemaphoreType.DMA,
        ],
        compiler_params=params,
        name="scaled_scatter_rows",
    )(table, *parts, back)


def fetch_kernel(after_ref, right_hbm, out_ref, sem):
    columns = right_hbm.at[:, pl.ds(0, out_ref.shape[1])]
    copy = pltpu.make_async_copy(columns, out_ref, sem)
    copy.start()
    copy.wait()


def fetch_columns(after, right, columns):
    return pl.pallas_call(
        fetch_kernel,
        out_shape=jax.ShapeDtypeStruct((right.shape[0], columns), jnp.bfloat16),
        in_specs=[VMEM, HBM],
        out_specs=VMEM,
        scratch_shapes=[pltpu.SemaphoreType.DMA],
        compiler_params=pltpu.CompilerParams(vmem_limit_bytes=8 * MIB),
        name="fetch_columns",
    )(after, in_hbm(right))


def owners(table_ref, half):
    table = table_ref[half]
    return jnp.concatenate([table[col : col + 1] for col in range(table.shape[0])], axis=1)


def block_kernel(half, table_ref, *refs):
    parts = len(refs) - 10
    part_refs = refs[:parts]
    rows_ref, first_ref, right_hbm, left_hbm, out_ref, right_ref, left_ref, mixed_ref, shaped_ref, sem = refs[parts:]
    block_size = right_hbm.shape[0]
    tile = first_ref.shape[1]
    loads = start_loads(right_hbm, left_hbm, right_ref, left_ref, tile, sem)
    totals = part_refs[0][...]
    for part_ref in part_refs[1:]:
        totals = totals + part_ref[...]
    adam_sq = jnp.sum(jnp.where(owners(table_ref, half) == lax.axis_index(DP), totals, 0.0))
    mix(rows_ref, first_ref, right_ref, mixed_ref, tile, loads)

    def shape(j, squares):
        cols = pl.ds(pl.multiple_of(j * tile, tile), tile)
        shaped = jnp.dot(left_ref[...], mixed_ref[:, cols], preferred_element_type=jnp.float32)
        shaped_ref[:, cols] = shaped
        return squares + jnp.sum((shaped * shaped).reshape(block_size // 8, 8, tile), axis=0)

    squares = lax.fori_loop(0, block_size // tile, shape, jnp.zeros((8, tile), jnp.float32))
    shaped_sq = jnp.full((8, 128), jnp.sum(squares), jnp.float32)
    scale = jnp.sqrt((adam_sq + NORM_EPS) / (shaped_sq + NORM_EPS))[0:1, 0:1]
    band = block_size // 4

    def finish(i, carry):
        rows = pl.ds(pl.multiple_of(i * band, band), band)
        out_ref[rows, :] = (shaped_ref[rows, :] * scale).astype(jnp.bfloat16)
        return carry

    lax.fori_loop(0, 4, finish, 0)


def raw_block_kernel(
    half, table_ref, rows_ref, first_ref, right_hbm, left_hbm, out_hbm, square_ref, right_ref, left_ref, mixed_ref, held_ref, sem
):
    block_size = right_hbm.shape[0]
    tile = first_ref.shape[1]
    steps = block_size // tile
    loads = start_loads(right_hbm, left_hbm, right_ref, left_ref, tile, sem)
    mix(rows_ref, first_ref, right_ref, mixed_ref, tile, loads)

    def store(j):
        cols = pl.ds(pl.multiple_of(j * tile, tile), tile)
        return pltpu.make_async_copy(held_ref.at[:, cols], out_hbm.at[:, cols], sem.at[j])

    def shape(j, squares):
        cols = pl.ds(pl.multiple_of(j * tile, tile), tile)
        shaped = jnp.dot(left_ref[...], mixed_ref[:, cols], preferred_element_type=jnp.float32)
        held_ref[:, cols] = shaped.astype(jnp.bfloat16)
        store(j).start()
        return squares + jnp.sum((shaped * shaped).reshape(block_size // 8, 8, tile), axis=0)

    squares = lax.fori_loop(0, steps, shape, jnp.zeros((8, tile), jnp.float32))
    square_ref[...] = jnp.where(owners(table_ref, half) == lax.axis_index(DP), jnp.sum(squares), 0.0)
    for j in range(steps):
        store(j).wait()


def start_loads(right_hbm, left_hbm, right_ref, left_ref, tile, sem):
    rest = pl.ds(tile, right_hbm.shape[1] - tile)
    right_load = pltpu.make_async_copy(right_hbm.at[:, rest], right_ref.at[:, rest], sem.at[0])
    left_load = pltpu.make_async_copy(left_hbm, left_ref, sem.at[1])
    right_load.start()
    left_load.start()
    return right_load, left_load


def mix(rows_ref, first_ref, right_ref, mixed_ref, tile, loads):
    for start in range(0, mixed_ref.shape[1], tile):
        cols = pl.ds(start, tile)
        if start == tile:
            loads[0].wait()
        columns = right_ref[:, cols] if start > 0 else first_ref[...]
        mixed = jnp.dot(rows_ref[...], columns, preferred_element_type=jnp.float32)
        mixed_ref[:, cols] = mixed.astype(jnp.bfloat16)
    loads[1].wait()


def own_block(rows_in, first, right, left, table, half, parts=()):
    block_size = right.shape[0]
    shape = (block_size, block_size)
    square = pltpu.VMEM(shape, jnp.bfloat16)
    finished = len(parts) > 0
    if finished:
        kernel, held = block_kernel, pltpu.VMEM(shape, jnp.float32)
        out_shape = jax.ShapeDtypeStruct(shape, jnp.bfloat16)
    else:
        kernel, held = raw_block_kernel, square
        out_shape = (pltpu.HBM(shape, jnp.bfloat16), jax.ShapeDtypeStruct((1, table[0].size), jnp.float32))
    return pl.pallas_call(
        functools.partial(kernel, half),
        out_shape=out_shape,
        in_specs=[VMEM] * (len(parts) + 3) + [HBM] * 2,
        out_specs=VMEM if finished else (HBM, VMEM),
        scratch_shapes=[square, square, square, held, pltpu.SemaphoreType.DMA((2,))],
        compiler_params=pltpu.CompilerParams(vmem_limit_bytes=24 * MIB),
        name="own_block" if finished else "raw_block",
        cost_estimate=pl.CostEstimate(
            flops=4 * block_size**3, bytes_accessed=8 * block_size**2, transcendentals=0
        ),
    )(table, *parts, rows_in, first, in_hbm(right), in_hbm(left))


def exchange(value):
    return lax.all_to_all(value, DP, split_axis=0, concat_axis=0, tiled=True)


def adam_sums(grad, second_moment, block_size):
    row_blocks, block_rows, half_cols = grad.shape
    col_blocks = half_cols // block_size
    widened = grad.astype(jnp.float32)
    moment_new = BETA_TWO * second_moment + (1.0 - BETA_TWO) * widened * widened
    direction = widened / (jnp.sqrt(moment_new) + ADAM_EPS)
    sums = jnp.sum(
        (direction * direction).reshape(row_blocks, block_rows, col_blocks, block_size), axis=(1, 3)
    )
    return jnp.transpose(sums).reshape(1, row_blocks * col_blocks)


def plane_sums(value):
    return lax.psum(lax.psum(value, "dp_0"), "dp_2")


def all_planes(plane):
    depth = lax.axis_size("dp_1")
    parts = [plane]
    for step in range(1, depth):
        ring = [(i, (i + step) % depth) for i in range(depth)]
        parts.append(lax.ppermute(plane, "dp_1", ring))
    return parts


def first_core(grad, second_moment, left, right, table):
    block_size = left.shape[0]
    slots = lax.axis_size(DP)
    outgoing, first = gather_rows(table, grad, 0, slots, block_size, right)
    rows_in = exchange(outgoing)
    result, square = own_block(
        rows_in.reshape(block_size, block_size), first, right, left, table, 0
    )
    second_moment, result = lax.optimization_barrier((second_moment, result))
    back = exchange(result.reshape(outgoing.shape))
    sums = jnp.concatenate([adam_sums(grad, second_moment, block_size), square], axis=0)
    return scatter_rows(table, back, 0, grad, all_planes(plane_sums(sums)))


def second_core(grad, second_moment, left, right, table):
    block_size = left.shape[0]
    outgoing = gather_rows(table, grad, 1, lax.axis_size(DP), block_size)
    parts = all_planes(plane_sums(adam_sums(grad, second_moment, block_size)))
    *parts[:3], outgoing = lax.optimization_barrier((*parts[:3], outgoing))
    rows_in = exchange(outgoing)
    first = fetch_columns(parts[-1], right, block_size // 2)
    result = own_block(
        rows_in.reshape(block_size, block_size), first, right, left, table, 1, parts
    )
    back = exchange(result.reshape(outgoing.shape))
    return scatter_rows(table, back, 1, grad)


def per_device(grad, second_moment, left_root, right_root, owner_slot):
    table = jnp.transpose(owner_slot, (0, 2, 1))
    return lax.cond(
        lax.axis_index("mp") == 0,
        first_core,
        second_core,
        grad,
        second_moment,
        left_root[0, 0],
        right_root[0, 0],
        table,
    )


def solution(mesh):
    split = Mesh(mesh.devices.reshape(4, 8, 4, mesh.shape["mp"]), ("dp_0", "dp_1", "dp_2", "mp"))
    return jax.shard_map(
        per_device,
        mesh=split,
        in_specs=(
            P(None, DP, "mp"),
            P(None, DP, "mp"),
            P("mp", DP, None, None),
            P("mp", DP, None, None),
            P(),
        ),
        out_specs=P(None, DP, "mp"),
        check_vma=False,
    )
```

time: 122 us -> 121 us (level)
    all_to_all x1, waiting for transfers between devices: 3.99 us -> 1.9 us  [exchange(): return lax.all_to_all(value, DP, split_axis=0, concat_axis=0, tiled=True)]
    ppermute x7, waiting for transfers between devices: 17.1 us -> 19.1 us  [all_planes(): parts.append(lax.ppermute(plane, 'dp_1', ring))]
  transfers between devices with their start and end apart: 8 -> 8, of which waited for: 5 -> 6; matrix products, arithmetic and copies ran while one was open for 0% -> 0% of each run, Pallas kernels for 3% -> 3%
where the time goes in v5:
time: 121 us
  blocking collectives  57.9 us (48%)
  starting transfers between devices  22.5 us (19%)
  waiting for transfers between devices  21 us (17%)
  Pallas kernels  11.9 us (10%)
  other arithmetic  6.16 us (5%)
    all_to_all x1, blocking collectives, exchange(): return lax.all_to_all(value, DP, split_axis=0, concat_axis=0, tiled=True)  39.1 us
    ppermute x7, waiting for transfers between devices, all_planes(): parts.append(lax.ppermute(plane, 'dp_1', ring))  19.1 us
    psum x2, blocking collectives, plane_sums(): return lax.psum(lax.psum(value, 'dp_0'), 'dp_2')  18.8 us
    ppermute x7, starting transfers between devices, all_planes(): parts.append(lax.ppermute(plane, 'dp_1', ring))  14.2 us
    all_to_all x1, starting transfers between devices, exchange(): return lax.all_to_all(value, DP, split_axis=0, concat_axis=0, tiled=True)  8.24 us
    pallas_call x1, Pallas kernels, own_block(): pl.pallas_call(functools.partial(kernel, half), out_shape=out_shape, in_s...  6.45 us
    reduce_sum x2, other arithmetic, adam_sums(): jnp.sum((direction * direction).reshape(row_blocks, block_rows, col_block...  6.16 us
  transfers between devices with their start and end apart: 8, of which 6 were waited for; matrix products, arithmetic and copies ran while one was open for 0% of the time, Pallas kernels for 3%

profile of v5, /device:TPU:1, one launch (start us, length us, event | category | flops | bytes accessed | tf_op | source)
XLA Modules:
  0.0 120.8 jit_solution(16059238346579682657)
XLA Ops:
  0.0 120.6 %conditional.1 = (bf16[32,8,4096]{2,1,0:T(8,128)(2,1)}) conditional(s32[]{:T(128)} %convert_element_type.9, (bf16[32,8,4096]{2,1,0:T(8,128)(2,1)}, f32[32,8,4096]{2,1,0:T(8,128)}, s32[2,4,32]{2,1,0:T(4,128)}, bf16[1024,1024]{1,0:T(8,128)(2,1)}, bf16[1024,1024]{1,0:T(8,128)(2,1)}) %tuple.23, (bf16[32,8,4096]{2,1,0:T(8,128)(2,1)}, ...), branch_computations={%region_0.5_spmd, %region_5.10_spmd} | conditional | flops 4304404480 | bytes 27304800 | solution.py:355
  0.0 6.0 %fusion.4 = f32[32,4096]{1,0:T(8,128)S(1)} fusion(f32[32,8,4096]{2,1,0:T(8,128)} %get-tuple-element.30, bf16[32,8,4096]{2,1,0:T(8,128)(2,1)} %get-tuple-element.29.grad_hbm), kind=kLoop, calls=%fused_computation.6 | loop fusion | flops 9306112 | bytes 6815744 | tf_op jit(solution)/shard_map/cond/branch_0_fun/reduce_sum | solution.py:306
  6.0 0.4 reduce_sum.18
  6.4 0.1 reduce_sum.19
  6.5 0.1 copy.10
  6.6 0.1 reshape.16
  6.7 9.5 %psum.24 = f32[1,128]{1,0:T(1,128)S(1)} all-reduce(f32[1,128]{1,0:T(1,128)S(1)} %reshape.16), channel_id=1, replica_groups=mesh['dp_0'=4,'dp_1'=8,'dp_2'=4,'mp'=2] {'dp_0'}, use_global_device_ids=true, to_apply=%region_3.0 | all-reduce | flops 128 | bytes 1024 | tf_op jit(solution)/shard_map/cond/branch_0_fun/psum | solution.py:313
  16.2 9.3 %psum.25.refs_0_ = f32[1,128]{1,0:T(1,128)S(1)} all-reduce(f32[1,128]{1,0:T(1,128)S(1)} %psum.24), channel_id=1, replica_groups=mesh['dp_0'=4,'dp_1'=8,'dp_2'=4,'mp'=2] {'dp_2'}, use_global_device_ids=true, to_apply=%region_4.4 | all-reduce | flops 128 | bytes 1024 | tf_op jit(solution)/shard_map/cond/branch_0_fun/psum | solution.py:313
  25.5 3.4 %collective-permute-start = (f32[1,128]{1,0:T(1,128)S(1)}, f32[1,128]{1,0:T(1,128)S(1)}, u32[]{:S(2)}, u32[]{:S(2)}) collective-permute-start(f32[1,128]{1,0:T(1,128)S(1)} %psum.25.refs_0_), channel_id=1, source_target_pairs={{0,8},{8,16},{16,24},{24,32},{32,40},{40,48},{48,56},{56,0},{1,9},... | collective-permute-start | bytes 1544 | tf_op jit(solution)/shard_map/cond/branch_0_fun/ppermute | solution.py:321
  28.9 1.2 %collective-permute-start.1 = (f32[1,128]{1,0:T(1,128)S(1)}, f32[1,128]{1,0:T(1,128)S(1)}, u32[]{:S(2)}, u32[]{:S(2)}) collective-permute-start(f32[1,128]{1,0:T(1,128)S(1)} %psum.25.refs_0_), channel_id=1, source_target_pairs={{0,16},{8,24},{16,32},{24,40},{32,48},{40,56},{48,0},{56,8},{1,17}... | collective-permute-start | bytes 1544 | tf_op jit(solution)/shard_map/cond/branch_0_fun/ppermute | solution.py:321
  30.1 2.3 %gather_rows.2 = bf16[128,8,1024]{2,1,0:T(8,128)(2,1)} custom-call(s32[2,4,32]{2,1,0:T(4,128)} %get-tuple-element.28.table_hbm.table_ref, bf16[32,8,4096]{2,1,0:T(8,128)(2,1)} %get-tuple-element.29.grad_hbm), custom_call_target="tpu_custom_call" | custom-call | tf_op jit(solution)/shard_map/cond/branch_0_fun/gather_rows/pallas_call | solution.py:80
  32.4 0.0 copy-start
  32.4 0.6 collective-permute-done.refs_1_
  33.0 1.1 collective-permute-done.1.refs_2_
  34.1 8.2 %all-to-all-start = ((bf16[128,8,1024]{2,1,0:T(8,128)(2,1)}), bf16[128,8,1024]{2,1,0:T(8,128)(2,1)S(1)}, u32[]{:S(2)}, u32[]{:S(2)}) async-start(bf16[128,8,1024]{2,1,0:T(8,128)(2,1)} %gather_rows.2), calls=%async_computation | async-start | bytes 4194304 | tf_op jit(solution)/shard_map/cond/branch_0_fun/all_to_all | solution.py:297
  42.4 1.9 %collective-permute-start.6 = (f32[1,128]{1,0:T(1,128)S(1)}, f32[1,128]{1,0:T(1,128)S(1)}, u32[]{:S(2)}, u32[]{:S(2)}) collective-permute-start(f32[1,128]{1,0:T(1,128)S(1)} %psum.25.refs_0_), channel_id=1, source_target_pairs={{0,56},{8,0},{16,8},{24,16},{32,24},{40,32},{48,40},{56,48},{1,57}... | collective-permute-start | bytes 1544 | tf_op jit(solution)/shard_map/cond/branch_0_fun/ppermute | solution.py:321
  44.3 0.8 collective-permute-start.2
  45.1 3.3 %collective-permute-start.3 = (f32[1,128]{1,0:T(1,128)S(1)}, f32[1,128]{1,0:T(1,128)S(1)}, u32[]{:S(2)}, u32[]{:S(2)}) collective-permute-start(f32[1,128]{1,0:T(1,128)S(1)} %psum.25.refs_0_), channel_id=1, source_target_pairs={{0,32},{8,40},{16,48},{24,56},{32,0},{40,8},{48,16},{56,24},{1,33}... | collective-permute-start | bytes 1544 | tf_op jit(solution)/shard_map/cond/branch_0_fun/ppermute | solution.py:321
  48.4 3.3 %collective-permute-start.4 = (f32[1,128]{1,0:T(1,128)S(1)}, f32[1,128]{1,0:T(1,128)S(1)}, u32[]{:S(2)}, u32[]{:S(2)}) collective-permute-start(f32[1,128]{1,0:T(1,128)S(1)} %psum.25.refs_0_), channel_id=1, source_target_pairs={{0,40},{8,48},{16,56},{24,0},{32,8},{40,16},{48,24},{56,32},{1,41}... | collective-permute-start | bytes 1544 | tf_op jit(solution)/shard_map/cond/branch_0_fun/ppermute | solution.py:321
  51.7 0.3 collective-permute-start.5
  52.0 12.3 %collective-permute-done.6.after_ref.refs_7_ = f32[1,128]{1,0:T(1,128)S(1)} collective-permute-done((f32[1,128]{1,0:T(1,128)S(1)}, f32[1,128]{1,0:T(1,128)S(1)}, u32[]{:S(2)}, u32[]{:S(2)}) %collective-permute-start.6) | collective-permute-done | bytes 544 | tf_op jit(solution)/shard_map/cond/branch_0_fun/ppermute | solution.py:321
  64.3 1.2 %fetch_columns.1.refs_9_ = bf16[1024,512]{1,0:T(8,128)(2,1)S(1)} custom-call(f32[1,128]{1,0:T(1,128)S(1)} %collective-permute-done.6.after_ref.refs_7_, bf16[1024,1024]{1,0:T(8,128)(2,1)} %get-tuple-element.35.right_hbm.refs_10_), custom_call_target="tpu_custom_call" | custom-call | tf_op jit(solution)/shard_map/cond/branch_0_fun/fetch_columns/pallas_call | solution.py:177
  65.5 3.8 %collective-permute-done.2.refs_3_ = f32[1,128]{1,0:T(1,128)S(1)} collective-permute-done((f32[1,128]{1,0:T(1,128)S(1)}, f32[1,128]{1,0:T(1,128)S(1)}, u32[]{:S(2)}, u32[]{:S(2)}) %collective-permute-start.2) | collective-permute-done | bytes 544 | tf_op jit(solution)/shard_map/cond/branch_0_fun/ppermute | solution.py:321
  69.4 1.3 %collective-permute-done.3.refs_4_ = f32[1,128]{1,0:T(1,128)S(1)} collective-permute-done((f32[1,128]{1,0:T(1,128)S(1)}, f32[1,128]{1,0:T(1,128)S(1)}, u32[]{:S(2)}, u32[]{:S(2)}) %collective-permute-start.3) | collective-permute-done | bytes 544 | tf_op jit(solution)/shard_map/cond/branch_0_fun/ppermute | solution.py:321
  70.6 0.0 collective-permute-done.4.refs_5_
  70.6 0.0 collective-permute-done.5.refs_6_
  70.6 1.9 %all-to-all-done = bf16[128,8,1024]{2,1,0:T(8,128)(2,1)S(1)} async-done(((bf16[128,8,1024]{2,1,0:T(8,128)(2,1)}), bf16[128,8,1024]{2,1,0:T(8,128)(2,1)S(1)}, u32[]{:S(2)}, u32[]{:S(2)}) %all-to-all-start) | async-done | bytes 2097184 | tf_op jit(solution)/shard_map/cond/branch_0_fun/all_to_all | solution.py:297
  72.5 0.0 copy-done
  72.5 6.4 %own_block.1 = bf16[1024,1024]{1,0:T(8,128)(2,1)S(1)} custom-call(s32[2,4,32]{2,1,0:T(4,128)S(1)} %copy-done, f32[1,128]{1,0:T(1,128)S(1)} %psum.25.refs_0_, f32[1,128]{1,0:T(1,128)S(1)} %collective-permute-done.refs_1_, f32[1,128]{1,0:T(1,128)S(1)} %collective-permute-done.1.refs_2_, f32[1,128]{1,0:T(1,128)S(1)} %collective-permute-done.2.refs_3_, ...), custom_call_target="tpu_custom_call" | custom-call | flops 4294967296 | bytes 8388608 | tf_op jit(solution)/shard_map/cond/branch_0_fun/own_block/pallas_call | solution.py:282
  79.0 39.1 %all_to_all.16.back_ref = bf16[128,8,1024]{2,1,0:T(8,128)(2,1)S(1)} all-to-all(bf16[128,8,1024]{2,1,0:T(8,128)(2,1)S(1)} %bitcast.10), channel_id=1, replica_groups=mesh['dp_0'=4,'dp_1'=8,'dp_2'=4,'mp'=2] {'dp_0','dp_1','dp_2'}, dimensions={0} | all-to-all | bytes 4194304 | tf_op jit(solution)/shard_map/cond/branch_0_fun/all_to_all | solution.py:297
  118.1 1.9 %scatter_rows.1 = bf16[32,8,4096]{2,1,0:T(8,128)(2,1)} custom-call(s32[2,4,32]{2,1,0:T(4,128)S(1)} %copy-done, bf16[128,8,1024]{2,1,0:T(8,128)(2,1)S(1)} %all_to_all.16.back_ref), custom_call_target="tpu_custom_call" | custom-call | tf_op jit(solution)/shard_map/cond/branch_0_fun/scatter_rows/pallas_call | solution.py:144
Async XLA Ops:
  25.5 7.6 %collective-permute-start = (f32[1,128]{1,0:T(1,128)S(1)}, f32[1,128]{1,0:T(1,128)S(1)}, u32[]{:S(2)}, u32[]{:S(2)}) collective-permute-start(f32[1,128]{1,0:T(1,128)S(1)} %psum.25.refs_0_), channel_id=1, source_target_pairs={{0,8},{8,16},{16,24},{24,32},{32,40},{40,48},{48,56},{56,0},{1,9},... | collective-permute-start | bytes 1544 | tf_op jit(solution)/shard_map/cond/branch_0_fun/ppermute | solution.py:321
  28.9 5.3 %collective-permute-start.1 = (f32[1,128]{1,0:T(1,128)S(1)}, f32[1,128]{1,0:T(1,128)S(1)}, u32[]{:S(2)}, u32[]{:S(2)}) collective-permute-start(f32[1,128]{1,0:T(1,128)S(1)} %psum.25.refs_0_), channel_id=1, source_target_pairs={{0,16},{8,24},{16,32},{24,40},{32,48},{40,56},{48,0},{56,8},{1,17}... | collective-permute-start | bytes 1544 | tf_op jit(solution)/shard_map/cond/branch_0_fun/ppermute | solution.py:321
  32.4 40.1 %copy-start = (s32[2,4,32]{2,1,0:T(4,128)S(1)}, s32[2,4,32]{2,1,0:T(4,128)}, u32[]{:S(2)}) copy-start(s32[2,4,32]{2,1,0:T(4,128)} %get-tuple-element.28.table_hbm.table_ref) | copy-start | bytes 3076 | tf_op jit(solution)/shard_map/cond
  34.1 38.4 %all-to-all-start = ((bf16[128,8,1024]{2,1,0:T(8,128)(2,1)}), bf16[128,8,1024]{2,1,0:T(8,128)(2,1)S(1)}, u32[]{:S(2)}, u32[]{:S(2)}) async-start(bf16[128,8,1024]{2,1,0:T(8,128)(2,1)} %gather_rows.2), calls=%async_computation | async-start | bytes 4194304 | tf_op jit(solution)/shard_map/cond/branch_0_fun/all_to_all | solution.py:297
  42.4 21.9 %collective-permute-start.6 = (f32[1,128]{1,0:T(1,128)S(1)}, f32[1,128]{1,0:T(1,128)S(1)}, u32[]{:S(2)}, u32[]{:S(2)}) collective-permute-start(f32[1,128]{1,0:T(1,128)S(1)} %psum.25.refs_0_), channel_id=1, source_target_pairs={{0,56},{8,0},{16,8},{24,16},{32,24},{40,32},{48,40},{56,48},{1,57}... | collective-permute-start | bytes 1544 | tf_op jit(solution)/shard_map/cond/branch_0_fun/ppermute | solution.py:321
  44.3 25.1 %collective-permute-start.2 = (f32[1,128]{1,0:T(1,128)S(1)}, f32[1,128]{1,0:T(1,128)S(1)}, u32[]{:S(2)}, u32[]{:S(2)}) collective-permute-start(f32[1,128]{1,0:T(1,128)S(1)} %psum.25.refs_0_), channel_id=1, source_target_pairs={{0,24},{8,32},{16,40},{24,48},{32,56},{40,0},{48,8},{56,16},{1,25}... | collective-permute-start | bytes 1544 | tf_op jit(solution)/shard_map/cond/branch_0_fun/ppermute | solution.py:321
  45.1 25.6 %collective-permute-start.3 = (f32[1,128]{1,0:T(1,128)S(1)}, f32[1,128]{1,0:T(1,128)S(1)}, u32[]{:S(2)}, u32[]{:S(2)}) collective-permute-start(f32[1,128]{1,0:T(1,128)S(1)} %psum.25.refs_0_), channel_id=1, source_target_pairs={{0,32},{8,40},{16,48},{24,56},{32,0},{40,8},{48,16},{56,24},{1,33}... | collective-permute-start | bytes 1544 | tf_op jit(solution)/shard_map/cond/branch_0_fun/ppermute | solution.py:321
  48.4 22.2 %collective-permute-start.4 = (f32[1,128]{1,0:T(1,128)S(1)}, f32[1,128]{1,0:T(1,128)S(1)}, u32[]{:S(2)}, u32[]{:S(2)}) collective-permute-start(f32[1,128]{1,0:T(1,128)S(1)} %psum.25.refs_0_), channel_id=1, source_target_pairs={{0,40},{8,48},{16,56},{24,0},{32,8},{40,16},{48,24},{56,32},{1,41}... | collective-permute-start | bytes 1544 | tf_op jit(solution)/shard_map/cond/branch_0_fun/ppermute | solution.py:321
  51.7 19.0 %collective-permute-start.5 = (f32[1,128]{1,0:T(1,128)S(1)}, f32[1,128]{1,0:T(1,128)S(1)}, u32[]{:S(2)}, u32[]{:S(2)}) collective-permute-start(f32[1,128]{1,0:T(1,128)S(1)} %psum.25.refs_0_), channel_id=1, source_target_pairs={{0,48},{8,56},{16,0},{24,8},{32,16},{40,24},{48,32},{56,40},{1,49}... | collective-permute-start | bytes 1544 | tf_op jit(solution)/shard_map/cond/branch_0_fun/ppermute | solution.py:321
